TPU v7x, 256 devices: a whole 4x4x8 slice. The times are simulated.
256 devices in a mesh: gx: 8 (over y, core), gy: 4 (over x), gz: 8 (over z).
Axes of the slice: x: 4, y: 4, z: 8, core: 2. Of those that a mesh axis runs over, the one named last changes fastest.
Arguments:
- velocity: float32 [128, 64, 3, 1024], P('gx', 'gy', None, 'gz'), may hold values from -6 to 6
- marker_pos: float32 [16384, 3, 256], P(('gx', 'gy', 'gz')), may hold values from -130 to 256
- marker_force: float32 [16384, 3, 256], P(('gx', 'gy', 'gz')), may hold values from -6 to 6
- intersect: int32 [16384, 27], P(('gx', 'gy', 'gz')), may hold values from 0 to 1, as said below
- tiles: int32 [16384, 27, 16], P(('gx', 'gy', 'gz')), may hold values from 0 to 255, as said below
Outputs:
- velocity_out: float32 [128, 64, 3, 1024], P('gx', 'gy', None, 'gz')
- marker_velocity: float32 [16384, 3, 256], P(('gx', 'gy', 'gz'))
Inputs may be any that keep to these rules, and one draw needn't show every extreme that they name: `intersect`: column 13 is always 1. Of one owner's bubbles at most 16 have a 1 in any other column; on every draw some owner has exactly 16 in some column, and some device is intersected by exactly 16 bubbles of its neighbour at each of the 26 other offsets. tiles[b, q, j] is a tile of the device at offset q from b's owner, numbered ix * 16 + iy for the line of cells (ix, iy); entries of columns where intersect is 0 are not used.
All inputs are finite; a program needn't handle non-finite values.
Results may differ from a plain program's by a relative error of at most 0.0049.
Values sent between devices are 32-bit elements; how exact they have to be, the bound alone decides.
A program may use at most 128 MiB of HBM per device.

v0:
```python
import jax
import jax.numpy as jnp
import numpy as np
from jax import lax
from jax.sharding import PartitionSpec as P

CAP = 16


spread_width = 0.5
viscous = 0.1
row_block = 32


def passed_along(value, axis, steps):
    count = lax.axis_size(axis)
    pairs = [(source, (source + steps) % count) for source in range(count)]
    return lax.ppermute(value, axis, pairs)


def padded_2(x, sides, width):
    edges = {}
    for axis, dim in sides:
        devices, length = (lax.axis_size(axis), x.shape[dim])
        up = [(i, (i + 1) % devices) for i in range(devices)]
        last = lax.slice_in_dim(x, length - width, length, axis=dim)
        initial = lax.slice_in_dim(x, 0, width, axis=dim)
        edges[dim] = (
            lax.ppermute(last, axis, up),
            lax.ppermute(initial, axis, [(b, a) for a, b in up]),
        )
    done = []
    for _, dim in sides:
        low, high = edges[dim]
        around = [(width, width) if d in done else (0, 0) for d in range(x.ndim)]
        x = jnp.concatenate([jnp.pad(low, around), x, jnp.pad(high, around)], axis=dim)
        done.append(dim)
    return x


def offset_table():
    direction = jnp.arange(27, dtype=jnp.int32)
    return jnp.stack([direction // 9 - 1, direction // 3 % 3 - 1, direction % 3 - 1], axis=1)


def line_weights(rel_pos, tile_ids, size_y, tile_len):
    cell_z = jnp.arange(tile_len, dtype=jnp.int32).astype(jnp.float32)
    along_z = jnp.exp(
        -spread_width * jnp.square(cell_z[None, :, None] - rel_pos[:, 2, None, :])
    ).astype(jnp.bfloat16)
    tile_x = (tile_ids // size_y).astype(jnp.float32)
    tile_y = (tile_ids % size_y).astype(jnp.float32)
    across = jnp.exp(
        -spread_width
        * (
            jnp.square(tile_x[:, :, None] - rel_pos[:, None, 0, :])
            + jnp.square(tile_y[:, :, None] - rel_pos[:, None, 1, :])
        )
    )
    across = jnp.where(tile_ids[:, :, None] >= 0, across, jnp.zeros_like(across))
    return (along_z, across)


def compact(flag_cols, capacity):
    ranking = jnp.cumsum(flag_cols, axis=0) - 1
    slot_ids = jnp.arange(capacity, dtype=jnp.int32)
    matches = (ranking.T[:, None, :] == slot_ids[None, :, None]) & (flag_cols.T[:, None, :] == 1)
    bubble = jnp.arange(flag_cols.shape[0], dtype=jnp.int32)
    picked = jnp.sum(jnp.where(matches, bubble[None, None, :], 0), axis=2)
    return (matches, picked, jnp.any(matches, axis=2))


def relay_section(stacked, axis_dim, sender):
    forward_part = sender(lax.index_in_dim(stacked, 2, axis_dim), 1)
    backward_part = sender(lax.index_in_dim(stacked, 0, axis_dim), -1)
    middle = lax.index_in_dim(stacked, 1, axis_dim)
    return jnp.concatenate([backward_part, middle, forward_part], axis=axis_dim)


def relay_out(stacked):
    stacked = relay_section(
        stacked, 0, lambda plane_in, step_sign: passed_along(plane_in, "gx", step_sign)
    )
    stacked = relay_section(
        stacked, 1, lambda plane_in, step_sign: passed_along(plane_in, "gy", step_sign)
    )
    return relay_section(
        stacked, 2, lambda plane_in, step_sign: passed_along(plane_in, "gz", step_sign)
    )


def relay_back(stacked):
    stacked = relay_section(
        stacked, 0, lambda plane_in, step_sign: passed_along(plane_in, "gx", step_sign)
    )
    stacked = relay_section(
        stacked, 1, lambda plane_in, step_sign: passed_along(plane_in, "gy", step_sign)
    )
    return relay_section(
        stacked, 2, lambda plane_in, step_sign: passed_along(plane_in, "gz", step_sign)
    )


def body(velocity, marker_pos, marker_force, intersect, tiles):
    bubbles, _, markers = marker_pos.shape
    size_x, size_y, _, tile_len = velocity.shape
    touched = tiles.shape[2]
    capacity = CAP
    tile_total = size_x * size_y
    neighbor_codes = np.concatenate([np.arange(13), np.arange(14, 27)])
    direction = jnp.arange(27, dtype=jnp.int32)
    not_self = (direction != 13)[:, None]
    block_size = jnp.array([size_x, size_y, tile_len], jnp.float32)
    shifts = offset_table().astype(jnp.float32) * block_size[None, :]
    matches, picked, usable = compact(intersect, capacity)
    usable = usable & not_self
    own_data = jnp.concatenate([marker_pos, marker_force], axis=1)
    chosen = own_data[picked]
    chosen_tiles = jnp.where(usable[:, :, None], tiles[picked, direction[:, None]], -1).astype(
        jnp.float32
    )
    filler = jnp.full((27, capacity, markers - touched), -1.0, jnp.float32)
    tile_row = jnp.concatenate([chosen_tiles, filler], axis=2)[:, :, None, :]
    packed = jnp.concatenate([chosen, tile_row], axis=2).reshape(3, 3, 3, capacity, 7, markers)
    arrived = relay_out(packed).reshape(27, capacity, 7, markers)
    incoming = arrived[:, :, :6]
    in_tiles = arrived[:, :, 6, :touched].astype(jnp.int32)
    nearby = incoming[neighbor_codes]
    near_pos = nearby[:, :, :3] - shifts[neighbor_codes][:, None, :, None]
    row_pos = jnp.concatenate([marker_pos, near_pos.reshape(-1, 3, markers)], axis=0)
    row_force = jnp.concatenate([marker_force, nearby[:, :, 3:].reshape(-1, 3, markers)], axis=0)
    row_tiles = jnp.concatenate(
        [tiles[:, 13, :], in_tiles[neighbor_codes].reshape(-1, touched)], axis=0
    )
    turns = row_pos.shape[0] // row_block
    tile_index = jnp.arange(tile_total, dtype=jnp.int32)

    def blocked(array_in):
        return array_in.reshape((turns, row_block) + array_in.shape[1:])

    def spread_step(running, block_in):
        pos_part, force_part, tile_part = block_in
        along_z, across = line_weights(pos_part, tile_part, size_y, tile_len)
        scaled = (force_part[:, None, :, :] * across[:, :, None, :]).astype(jnp.bfloat16)
        pieces = jnp.einsum("rtkm,rcm->rtkc", scaled, along_z, preferred_element_type=jnp.float32)
        pieces = pieces.reshape(-1, 3 * tile_len)
        high_part = pieces.astype(jnp.bfloat16)
        low_part = (pieces - high_part.astype(jnp.float32)).astype(jnp.bfloat16)
        placing = (tile_index[:, None] == tile_part.reshape(-1)[None, :]).astype(jnp.bfloat16)
        added = jnp.dot(placing, high_part, preferred_element_type=jnp.float32) + jnp.dot(
            placing, low_part, preferred_element_type=jnp.float32
        )
        return (running + added, None)

    force_tiles, _ = lax.scan(
        spread_step,
        jnp.zeros((tile_total, 3 * tile_len), jnp.float32),
        (blocked(row_pos), blocked(row_force), blocked(row_tiles)),
    )
    force_grid = force_tiles.reshape(size_x, size_y, 3, tile_len)
    padded = padded_2(velocity, (("gx", 0), ("gy", 1), ("gz", 3)), 1)
    laplace = (
        padded[2:, 1:-1, :, 1:-1]
        + padded[:-2, 1:-1, :, 1:-1]
        + padded[1:-1, 2:, :, 1:-1]
        + padded[1:-1, :-2, :, 1:-1]
        + padded[1:-1, 1:-1, :, 2:]
        + padded[1:-1, 1:-1, :, :-2]
        - 6.0 * velocity
    )
    velocity_out = velocity + viscous * laplace + force_grid
    grid_low = velocity_out.reshape(tile_total, 3 * tile_len).astype(jnp.bfloat16)

    def sample_step(carry_in, block_in):
        pos_part, tile_part = block_in
        along_z, across = line_weights(pos_part, tile_part, size_y, tile_len)
        picking = (tile_part.reshape(-1)[:, None] == tile_index[None, :]).astype(jnp.bfloat16)
        local_u = jnp.dot(picking, grid_low, preferred_element_type=jnp.float32).astype(
            jnp.bfloat16
        )
        local_u = local_u.reshape(row_block, touched, 3, tile_len)
        sampled = jnp.einsum("rtkc,rcm->rtkm", local_u, along_z, preferred_element_type=jnp.float32)
        return (carry_in, jnp.sum(sampled * across[:, :, None, :], axis=1))

    _, partial_value = lax.scan(
        sample_step, jnp.float32(0.0), (blocked(row_pos), blocked(row_tiles))
    )
    partial_value = partial_value.reshape(-1, 3, markers)
    own_part = partial_value[:bubbles]
    their_part = partial_value[bubbles:].reshape(26, capacity, 3, markers)
    hollow = jnp.zeros((1, capacity, 3, markers), jnp.float32)
    complete = jnp.concatenate([their_part[:13], hollow, their_part[13:]], axis=0).reshape(
        3, 3, 3, capacity, 3, markers
    )[::-1, ::-1, ::-1]
    returned = relay_back(complete)[::-1, ::-1, ::-1]
    returned = returned.reshape(27, capacity, 3, markers)
    weights_back = (matches & not_self[:, :, None]).astype(jnp.float32)
    marker_velocity = own_part + jnp.einsum(
        "qsb,qskm->bkm", weights_back, returned, precision=lax.Precision.HIGHEST
    )
    return (velocity_out, marker_velocity)


def solution(mesh):
    placed = (
        P("gx", "gy", None, "gz"),
        P(("gx", "gy", "gz"), None, None),
        P(("gx", "gy", "gz"), None, None),
        P(("gx", "gy", "gz"), None),
        P(("gx", "gy", "gz"), None, None),
    )
    return jax.shard_map(
        body,
        mesh=mesh,
        in_specs=placed,
        out_specs=(P("gx", "gy", None, "gz"), P(("gx", "gy", "gz"), None, None)),
        check_vma=False,
    )
```

profile of v0, /device:TPU:54, one launch (start us, length us, event | category | flops | bytes accessed | tf_op | source)
XLA Modules:
  0.0 297.8 jit_solution(13347250797021159055)
XLA Ops:
  6.9 5.3 %gather_fusion.1 = s32[432,16]{1,0:T(8,128)S(1)} fusion(s32[64,27,16]{2,0,1:T(8,128)S(1)} %copy.189, s32[432]{0:T(512)S(1)} %reshape.385), kind=kCustom, calls=%fused_computation.1 | custom fusion | bytes 58752 | tf_op jit(solution)/shard_map/gather | solution.py:119
  12.9 2.9 gather_fusion
  15.7 2.7 fusion.43
  19.1 1.7 collective-permute-start.6
  21.2 11.7 %collective-permute-done.7 = f32[1,3,3,16,7,256]{5,3,4,2,1,0:T(8,128)S(1)} collective-permute-done((f32[1,3,3,16,7,256]{5,3,4,2,1,0:T(8,128)S(1)}, f32[1,3,3,16,7,256]{5,3,4,2,1,0:T(8,128)S(1)}, u32[]{:S(2)}, u32[]{:S(2)}) %collective-permute-start.7) | collective-permute-done | bytes 1032224 | tf_op jit(solution)/shard_map/ppermute | solution.py:18
  34.2 1.5 collective-permute-start.8
  40.5 18.3 %collective-permute-done.9 = f32[3,1,3,16,7,256]{5,3,4,2,1,0:T(8,128)S(1)} collective-permute-done((f32[3,1,3,16,7,256]{5,3,4,2,1,0:T(8,128)S(1)}, f32[3,1,3,16,7,256]{5,3,4,2,1,0:T(8,128)S(1)}, u32[]{:S(2)}, u32[]{:S(2)}) %collective-permute-start.9) | collective-permute-done | bytes 1032224 | tf_op jit(solution)/shard_map/ppermute | solution.py:18
  58.8 2.0 collective-permute-done.8
  61.2 1.3 fusion.77
  62.5 1.9 collective-permute-start.11
  64.5 1.4 fusion.83
  68.6 1.9 collective-permute-start.5
  71.6 3.9 %collective-permute-start.4 = (f32[16,16,3,1]{3,2,1,0:T(4,128)}, f32[16,16,3,1]{3,2,1,0:T(4,128)}, u32[]{:S(2)}, u32[]{:S(2)}) collective-permute-start(f32[16,16,3,1]{3,2,1,0:T(4,128)} %get-tuple-element.313), channel_id=1, source_target_pairs={{1,0},{2,1},{3,2},{4,3},{5,4},{6,5},{7,6},{0,7},{9,8},{10,9},{11,1... | collective-permute-start | bytes 9224 | tf_op jit(solution)/shard_map/ppermute | solution.py:30
  76.2 12.3 %collective-permute-done.11 = f32[3,3,1,16,7,256]{5,3,4,2,1,0:T(8,128)} collective-permute-done((f32[3,3,1,16,7,256]{5,3,4,2,1,0:T(8,128)}, f32[3,3,1,16,7,256]{5,3,4,2,1,0:T(8,128)}, u32[]{:S(2)}, u32[]{:S(2)}) %collective-permute-start.11) | collective-permute-done | bytes 1032224 | tf_op jit(solution)/shard_map/ppermute | solution.py:18
  88.5 1.7 collective-permute-done.10
  90.2 1.8 pad_maximum_fusion.2
  92.1 1.8 slice.282
  95.5 2.5 gather_fusion.3
  102.7 79.4 %while.27 = (s32[]{:T(128)}, f32[256,384]{1,0:T(8,128)S(1)}, s32[15,32,16]{2,1,0:T(8,128)}, f32[15,32,3,256]{3,1,0,2:T(8,128)}, f32[15,32,3,256]{3,1,2,0:T(8,128)}, /*index=5*/s32[]{:T(128)}, s32[]{:T(128)}) while((s32[]{:T(128)}, f32[256,384]{1,0:T(8,128)S(1)}, s32[15,32,16]{2,1,0:T(8,128)}, f32[15,32,3,256]{3,1,0,2:T(8,128)}, ...), condition=%wide.region_4.5_spmd.clone, body=%wide.region_3.4_spmd.clone.sunk | while | flops 309243008 | bytes 7561323 | solution.py:155
  182.4 3.2 %fusion.75 = (bf16[16,16,3,128]{3,2,1,0:T(4,128)(2,1)S(1)}, f32[16,16,3,128]{3,2,1,0:T(4,128)S(1)}) fusion(f32[16,16,3,128]{3,2,1,0:T(4,128)S(1)} %reshape.374, f32[16,16,3,128]{3,2,1,0:T(4,128)S(1)} %copy.181, f32[18,1,3,128]{3,2,1,0:T(4,128)S(1)} %pad.15, f32[18,16,3,128]{3,2,1,0:T(4,128)S(1)} %copy-done.4, f32[18,1,3,128]{3,2,1,0:T(4,128)S(1)} %copy-done.5, ...), kind=kLoop, calls=%fused_computation.168 | loop fusion | flops 2654208 | bytes 1929216 | tf_op jit(solution)/shard_map/convert_element_type | solution.py:172
  185.7 66.1 %while.26 = (s32[]{:T(128)}, f32[15,32,3,256]{3,2,1,0:T(4,128)}, s32[15,32,16]{2,1,0:T(8,128)}, bf16[256,384]{1,0:T(8,128)(2,1)S(1)}, f32[15,32,3,256]{3,1,2,0:T(8,128)}, /*index=5*/s32[]{:T(128)}) while((s32[]{:T(128)}, f32[15,32,3,256]{3,2,1,0:T(4,128)}, s32[15,32,16]{2,1,0:T(8,128)}, bf16[256,384]{1,0:T(8,128)(2,1)S(1)}, ...), condition=%wide.region_7.8_spmd.clone, body=%wide.region_5.7_spmd.clone.sunk | while | flops 207539328 | bytes 3659865 | solution.py:185
  251.8 1.7 slice.225
  254.9 1.8 collective-permute-start.12
  257.8 5.0 %collective-permute-done.13 = f32[1,3,3,16,3,256]{5,3,4,2,1,0:T(8,128)} collective-permute-done((f32[1,3,3,16,3,256]{5,3,4,2,1,0:T(8,128)}, f32[1,3,3,16,3,256]{5,3,4,2,1,0:T(8,128)}, u32[]{:S(2)}, u32[]{:S(2)}) %collective-permute-start.13) | collective-permute-done | bytes 442400 | tf_op jit(solution)/shard_map/ppermute | solution.py:18
  262.8 1.3 pad_maximum_fusion.5
  264.6 1.7 collective-permute-start.14
  266.3 10.8 %collective-permute-done.15 = f32[3,1,3,16,3,256]{5,3,4,2,1,0:T(8,128)S(1)} collective-permute-done((f32[3,1,3,16,3,256]{5,3,4,2,1,0:T(8,128)S(1)}, f32[3,1,3,16,3,256]{5,3,4,2,1,0:T(8,128)S(1)}, u32[]{:S(2)}, u32[]{:S(2)}) %collective-permute-start.15) | collective-permute-done | bytes 442400 | tf_op jit(solution)/shard_map/ppermute | solution.py:18
  277.1 1.7 collective-permute-done.14
  279.0 3.0 %collective-permute-start.17 = (f32[3,3,1,16,3,256]{5,3,4,2,1,0:T(8,128)S(1)}, f32[3,3,1,16,3,256]{5,3,4,2,1,0:T(8,128)S(1)}, u32[]{:S(2)}, u32[]{:S(2)}) collective-permute-start(f32[3,3,1,16,3,256]{5,3,4,2,1,0:T(8,128)S(1)} %get-tuple-element.308), channel_id=1, source_target_pairs={{0,1},{1,2},{2,3},{3,4},{4,5},{5,6},{6,7},{7,0},{8,9},{9,10},{10,1... | collective-permute-start | bytes 1327112 | tf_op jit(solution)/shard_map/ppermute | solution.py:18
  283.9 7.9 %collective-permute-done.17 = f32[3,3,1,16,3,256]{5,3,4,2,1,0:T(8,128)S(1)} collective-permute-done((f32[3,3,1,16,3,256]{5,3,4,2,1,0:T(8,128)S(1)}, f32[3,3,1,16,3,256]{5,3,4,2,1,0:T(8,128)S(1)}, u32[]{:S(2)}, u32[]{:S(2)}) %collective-permute-start.17) | collective-permute-done | bytes 442400 | tf_op jit(solution)/shard_map/ppermute | solution.py:18
  291.8 3.7 %collective-permute-done.16 = f32[3,3,1,16,3,256]{5,3,4,2,1,0:T(8,128)S(1)} collective-permute-done((f32[3,3,1,16,3,256]{5,3,4,2,1,0:T(8,128)S(1)}, f32[3,3,1,16,3,256]{5,3,4,2,1,0:T(8,128)S(1)}, u32[]{:S(2)}, u32[]{:S(2)}) %collective-permute-start.16) | collective-permute-done | bytes 442400 | tf_op jit(solution)/shard_map/ppermute | solution.py:18
  295.7 2.1 fusion.47
  (484 shorter events, 174.5 us)
Async XLA Ops:
  12.2 0.7 copy-start.13
  18.8 14.1 %collective-permute-start.7 = (f32[1,3,3,16,7,256]{5,3,4,2,1,0:T(8,128)S(1)}, f32[1,3,3,16,7,256]{5,3,4,2,1,0:T(8,128)S(1)}, u32[]{:S(2)}, u32[]{:S(2)}) collective-permute-start(f32[1,3,3,16,7,256]{5,3,4,2,1,0:T(8,128)S(1)} %bitcast.197), channel_id=1, source_target_pairs={{0,32},{32,64},{64,96},{96,128},{128,160},{160,192},{192,224},{224... | collective-permute-start | bytes 3096584 | tf_op jit(solution)/shard_map/ppermute | solution.py:18
  19.1 13.9 %collective-permute-start.6 = (f32[1,3,3,16,7,256]{5,3,4,2,1,0:T(8,128)S(1)}, f32[1,3,3,16,7,256]{5,3,4,2,1,0:T(8,128)S(1)}, u32[]{:S(2)}, u32[]{:S(2)}) collective-permute-start(f32[1,3,3,16,7,256]{5,3,4,2,1,0:T(8,128)S(1)} %bitcast.198), channel_id=1, source_target_pairs={{0,224},{32,0},{64,32},{96,64},{128,96},{160,128},{192,160},{224,1... | collective-permute-start | bytes 3096584 | tf_op jit(solution)/shard_map/ppermute | solution.py:18
  33.3 2.4 copy-start
  33.6 25.2 %collective-permute-start.9 = (f32[3,1,3,16,7,256]{5,3,4,2,1,0:T(8,128)S(1)}, f32[3,1,3,16,7,256]{5,3,4,2,1,0:T(8,128)S(1)}, u32[]{:S(2)}, u32[]{:S(2)}) collective-permute-start(f32[3,1,3,16,7,256]{5,3,4,2,1,0:T(8,128)S(1)} %get-tuple-element.299), channel_id=1, source_target_pairs={{0,8},{8,16},{16,24},{24,0},{1,9},{9,17},{17,25},{25,1},{2,10},{10... | collective-permute-start | bytes 3096584 | tf_op jit(solution)/shard_map/ppermute | solution.py:18
  34.2 26.6 %collective-permute-start.8 = (f32[3,1,3,16,7,256]{5,3,4,2,1,0:T(8,128)S(1)}, f32[3,1,3,16,7,256]{5,3,4,2,1,0:T(8,128)S(1)}, u32[]{:S(2)}, u32[]{:S(2)}) collective-permute-start(f32[3,1,3,16,7,256]{5,3,4,2,1,0:T(8,128)S(1)} %get-tuple-element.298), channel_id=1, source_target_pairs={{0,24},{8,0},{16,8},{24,16},{1,25},{9,1},{17,9},{25,17},{2,26},{10... | collective-permute-start | bytes 3096584 | tf_op jit(solution)/shard_map/ppermute | solution.py:18
  36.6 31.4 %collective-permute-start.2 = (f32[16,1,3,128]{3,2,1,0:T(4,128)}, f32[16,1,3,128]{3,2,1,0:T(4,128)S(1)}, u32[]{:S(2)}, u32[]{:S(2)}) collective-permute-start(f32[16,1,3,128]{3,2,1,0:T(4,128)} %get-tuple-element.316), channel_id=1, source_target_pairs={{8,0},{16,8},{24,16},{0,24},{9,1},{17,9},{25,17},{1,25},{10,2},{18... | collective-permute-start | bytes 73736 | tf_op jit(solution)/shard_map/ppermute | solution.py:30
  38.0 29.3 %collective-permute-start.1 = (f32[1,16,3,128]{3,2,1,0:T(4,128)}, f32[1,16,3,128]{3,2,1,0:T(4,128)S(1)}, u32[]{:S(2)}, u32[]{:S(2)}) collective-permute-start(f32[1,16,3,128]{3,2,1,0:T(4,128)} %get-tuple-element.318), channel_id=1, source_target_pairs={{0,32},{32,64},{64,96},{96,128},{128,160},{160,192},{192,224},{224... | collective-permute-start | bytes 73736 | tf_op jit(solution)/shard_map/ppermute | solution.py:29
  38.8 37.4 %collective-permute-start = (f32[1,16,3,128]{3,2,1,0:T(4,128)}, f32[1,16,3,128]{3,2,1,0:T(4,128)S(1)}, u32[]{:S(2)}, u32[]{:S(2)}) collective-permute-start(f32[1,16,3,128]{3,2,1,0:T(4,128)} %get-tuple-element.317), channel_id=1, source_target_pairs={{32,0},{64,32},{96,64},{128,96},{160,128},{192,160},{224,192},{0,2... | collective-permute-start | bytes 73736 | tf_op jit(solution)/shard_map/ppermute | solution.py:30
  62.5 3.4 %copy-start.12 = (f32[3]{0:T(128)S(1)}, f32[3]{0:T(128)}, u32[]{:S(2)}) copy-start(f32[3]{0:T(128)} %constant.203.clone) | copy-start | bytes 40
  62.5 26.0 %collective-permute-start.11 = (f32[3,3,1,16,7,256]{5,3,4,2,1,0:T(8,128)}, f32[3,3,1,16,7,256]{5,3,4,2,1,0:T(8,128)}, u32[]{:S(2)}, u32[]{:S(2)}) collective-permute-start(f32[3,3,1,16,7,256]{5,3,4,2,1,0:T(8,128)} %get-tuple-element.296), channel_id=1, source_target_pairs={{0,1},{1,2},{2,3},{3,4},{4,5},{5,6},{6,7},{7,0},{8,9},{9,10},{10,1... | collective-permute-start | bytes 3096584 | tf_op jit(solution)/shard_map/ppermute | solution.py:18
  64.4 25.8 %collective-permute-start.10 = (f32[3,3,1,16,7,256]{5,3,4,2,1,0:T(8,128)S(1)}, f32[3,3,1,16,7,256]{5,3,4,2,1,0:T(8,128)}, u32[]{:S(2)}, u32[]{:S(2)}) collective-permute-start(f32[3,3,1,16,7,256]{5,3,4,2,1,0:T(8,128)S(1)} %get-tuple-element.295), channel_id=1, source_target_pairs={{0,7},{1,0},{2,1},{3,2},{4,3},{5,4},{6,5},{7,6},{8,15},{9,8},{10,9... | collective-permute-start | bytes 3096584 | tf_op jit(solution)/shard_map/ppermute | solution.py:18
  67.4 24.7 %copy-start.6 = (f32[1,16,3,128]{3,2,1,0:T(4,128)}, f32[1,16,3,128]{3,2,1,0:T(4,128)S(1)}, u32[]{:S(2)}) copy-start(f32[1,16,3,128]{3,2,1,0:T(4,128)S(1)} %collective-permute-done.1) | copy-start | bytes 73732
  67.4 4.2 %collective-permute-start.3 = (f32[16,1,3,128]{3,2,1,0:T(4,128)}, f32[16,1,3,128]{3,2,1,0:T(4,128)S(1)}, u32[]{:S(2)}, u32[]{:S(2)}) collective-permute-start(f32[16,1,3,128]{3,2,1,0:T(4,128)} %get-tuple-element.315), channel_id=1, source_target_pairs={{0,8},{8,16},{16,24},{24,0},{1,9},{9,17},{17,25},{25,1},{2,10},{10... | collective-permute-start | bytes 73736 | tf_op jit(solution)/shard_map/ppermute | solution.py:29
  68.0 0.6 copy-start.10
  68.6 113.7 %collective-permute-start.5 = (f32[16,16,3,1]{3,2,1,0:T(4,128)}, f32[16,16,3,1]{3,2,1,0:T(4,128)}, u32[]{:S(2)}, u32[]{:S(2)}) collective-permute-start(f32[16,16,3,1]{3,2,1,0:T(4,128)} %get-tuple-element.314), channel_id=1, source_target_pairs={{0,1},{1,2},{2,3},{3,4},{4,5},{5,6},{6,7},{7,0},{8,9},{9,10},{10,1... | collective-permute-start | bytes 9224 | tf_op jit(solution)/shard_map/ppermute | solution.py:29
  71.6 110.8 %collective-permute-start.4 = (f32[16,16,3,1]{3,2,1,0:T(4,128)}, f32[16,16,3,1]{3,2,1,0:T(4,128)}, u32[]{:S(2)}, u32[]{:S(2)}) collective-permute-start(f32[16,16,3,1]{3,2,1,0:T(4,128)} %get-tuple-element.313), channel_id=1, source_target_pairs={{1,0},{2,1},{3,2},{4,3},{5,4},{6,5},{7,6},{0,7},{9,8},{10,9},{11,1... | collective-permute-start | bytes 9224 | tf_op jit(solution)/shard_map/ppermute | solution.py:30
  76.2 15.9 %copy-start.8 = (f32[1,16,3,128]{3,2,1,0:T(4,128)}, f32[1,16,3,128]{3,2,1,0:T(4,128)S(1)}, u32[]{:S(2)}) copy-start(f32[1,16,3,128]{3,2,1,0:T(4,128)S(1)} %collective-permute-done) | copy-start | bytes 73732
  76.2 14.0 %copy-start.3 = (f32[18,16,3,128]{3,2,1,0:T(4,128)}, f32[18,16,3,128]{3,2,1,0:T(4,128)S(1)}, u32[]{:S(2)}) copy-start(f32[18,16,3,128]{3,2,1,0:T(4,128)S(1)} %constant_dynamic-update-slice_fusion) | copy-start | bytes 1327108
  98.2 0.9 copy-start.1
  100.4 0.9 copy-start.2
  102.7 79.6 %copy-start.4 = (f32[18,16,3,128]{3,2,1,0:T(4,128)S(1)}, f32[18,16,3,128]{3,2,1,0:T(4,128)}, u32[]{:S(2)}) copy-start(f32[18,16,3,128]{3,2,1,0:T(4,128)} %copy-done.3) | copy-start | bytes 1327108
  102.7 79.6 %copy-start.5 = (f32[18,1,3,128]{3,2,1,0:T(4,128)S(1)}, f32[18,1,3,128]{3,2,1,0:T(4,128)}, u32[]{:S(2)}) copy-start(f32[18,1,3,128]{3,2,1,0:T(4,128)} %pad.16) | copy-start | bytes 82948
  102.7 79.7 %copy-start.7 = (f32[1,16,3,128]{3,2,1,0:T(4,128)S(1)}, f32[1,16,3,128]{3,2,1,0:T(4,128)}, u32[]{:S(2)}) copy-start(f32[1,16,3,128]{3,2,1,0:T(4,128)} %copy-done.6) | copy-start | bytes 73732
  102.7 79.7 %copy-start.9 = (f32[1,16,3,128]{3,2,1,0:T(4,128)S(1)}, f32[1,16,3,128]{3,2,1,0:T(4,128)}, u32[]{:S(2)}) copy-start(f32[1,16,3,128]{3,2,1,0:T(4,128)} %copy-done.8) | copy-start | bytes 73732
  254.8 8.0 %collective-permute-start.13 = (f32[1,3,3,16,3,256]{5,3,4,2,1,0:T(8,128)}, f32[1,3,3,16,3,256]{5,3,4,2,1,0:T(8,128)}, u32[]{:S(2)}, u32[]{:S(2)}) collective-permute-start(f32[1,3,3,16,3,256]{5,3,4,2,1,0:T(8,128)} %slice.236), channel_id=1, source_target_pairs={{0,32},{32,64},{64,96},{96,128},{128,160},{160,192},{192,224},{224... | collective-permute-start | bytes 1327112 | tf_op jit(solution)/shard_map/ppermute | solution.py:18
  254.9 7.9 %collective-permute-start.12 = (f32[1,3,3,16,3,256]{5,3,4,2,1,0:T(8,128)S(1)}, f32[1,3,3,16,3,256]{5,3,4,2,1,0:T(8,128)}, u32[]{:S(2)}, u32[]{:S(2)}) collective-permute-start(f32[1,3,3,16,3,256]{5,3,4,2,1,0:T(8,128)S(1)} %slice.228), channel_id=1, source_target_pairs={{0,224},{32,0},{64,32},{96,64},{128,96},{160,128},{192,160},{224,1... | collective-permute-start | bytes 1327112 | tf_op jit(solution)/shard_map/ppermute | solution.py:18
  256.9 0.7 copy-start.11
  264.2 12.9 %collective-permute-start.15 = (f32[3,1,3,16,3,256]{5,3,4,2,1,0:T(8,128)S(1)}, f32[3,1,3,16,3,256]{5,3,4,2,1,0:T(8,128)S(1)}, u32[]{:S(2)}, u32[]{:S(2)}) collective-permute-start(f32[3,1,3,16,3,256]{5,3,4,2,1,0:T(8,128)S(1)} %get-tuple-element.311), channel_id=1, source_target_pairs={{0,8},{8,16},{16,24},{24,0},{1,9},{9,17},{17,25},{25,1},{2,10},{10... | collective-permute-start | bytes 1327112 | tf_op jit(solution)/shard_map/ppermute | solution.py:18
  264.6 14.2 %collective-permute-start.14 = (f32[3,1,3,16,3,256]{5,3,4,2,1,0:T(8,128)S(1)}, f32[3,1,3,16,3,256]{5,3,4,2,1,0:T(8,128)S(1)}, u32[]{:S(2)}, u32[]{:S(2)}) collective-permute-start(f32[3,1,3,16,3,256]{5,3,4,2,1,0:T(8,128)S(1)} %get-tuple-element.310), channel_id=1, source_target_pairs={{0,24},{8,0},{16,8},{24,16},{1,25},{9,1},{17,9},{25,17},{2,26},{10... | collective-permute-start | bytes 1327112 | tf_op jit(solution)/shard_map/ppermute | solution.py:18
  279.0 12.7 %collective-permute-start.17 = (f32[3,3,1,16,3,256]{5,3,4,2,1,0:T(8,128)S(1)}, f32[3,3,1,16,3,256]{5,3,4,2,1,0:T(8,128)S(1)}, u32[]{:S(2)}, u32[]{:S(2)}) collective-permute-start(f32[3,3,1,16,3,256]{5,3,4,2,1,0:T(8,128)S(1)} %get-tuple-element.308), channel_id=1, source_target_pairs={{0,1},{1,2},{2,3},{3,4},{4,5},{5,6},{6,7},{7,0},{8,9},{9,10},{10,1... | collective-permute-start | bytes 1327112 | tf_op jit(solution)/shard_map/ppermute | solution.py:18
  282.1 13.4 %collective-permute-start.16 = (f32[3,3,1,16,3,256]{5,3,4,2,1,0:T(8,128)S(1)}, f32[3,3,1,16,3,256]{5,3,4,2,1,0:T(8,128)S(1)}, u32[]{:S(2)}, u32[]{:S(2)}) collective-permute-start(f32[3,3,1,16,3,256]{5,3,4,2,1,0:T(8,128)S(1)} %get-tuple-element.307), channel_id=1, source_target_pairs={{0,7},{1,0},{2,1},{3,2},{4,3},{5,4},{6,5},{7,6},{8,15},{9,8},{10,9... | collective-permute-start | bytes 1327112 | tf_op jit(solution)/shard_map/ppermute | solution.py:18
where the time goes:
time: 301 us; the launch traced here: 298 us
  local copies, waits for them, and re-layouts  101 us (34%)
  waiting for transfers between devices  75.5 us (25%)
  matrix products  52.8 us (18%)
  other arithmetic  44.4 us (15%)
  starting transfers between devices  21.6 us (7%)
    ppermute x12, waiting for transfers between devices, passed_along(): return lax.ppermute(value, axis, pairs)  75.2 us
    squeeze x30, local copies, waits for them, and re-layouts, body(): lax.scan(spread_step, jnp.zeros((tile_total, 3 * tile_len), jnp.float32),...  27.1 us
    ge x30, other arithmetic, line_weights(): tile_ids[:, :, None] >= 0  21.9 us
    dot_general x15, matrix products, sample_step(): jnp.einsum('rtkc,rcm->rtkm', local_u, along_z, preferred_element_type=jnp...  18.3 us
    dot_general x15, matrix products, spread_step(): jnp.einsum('rtkm,rcm->rtkc', scaled, along_z, preferred_element_type=jnp....  16.8 us
    dynamic_slice x30, local copies, waits for them, and re-layouts, body(): lax.scan(spread_step, jnp.zeros((tile_total, 3 * tile_len), jnp.float32),...  14.7 us
    ppermute x12, starting transfers between devices, passed_along(): return lax.ppermute(value, axis, pairs)  12.8 us
    unnamed x43, local copies, waits for them, and re-layouts  10.7 us
  transfers between devices with their start and end apart: 18, of which 12 were waited for; matrix products, arithmetic and copies ran while one was open for 34% of the time, Pallas kernels for 0%

commit v1 on v0

v1 whole, which is shorter than its diff:
```python
import functools

import jax
import jax.numpy as jnp
from jax import lax
from jax.experimental import pallas as pl
from jax.experimental.pallas import tpu as pltpu
from jax.sharding import PartitionSpec as P

MESH = pl.DeviceIdType.MESH
CAP = 16
NEAR = 26
CHUNKS = 30
STEP = 5
LOG2E = 1.4426950408889634
ROOT = (0.5 * LOG2E) ** 0.5
F32 = jnp.float32
BF16 = jnp.bfloat16


def code_of(chunk):
    return (13 + STEP * jnp.minimum(chunk + 1, 27)) % 27


def offsets_of(chunk):
    code = code_of(chunk)
    return code // 9 - 1, code // 3 % 3 - 1, code % 3 - 1


def static_offsets(chunk):
    code = (13 + STEP * min(chunk + 1, 27)) % 27
    return code // 9 - 1, code // 3 % 3 - 1, code % 3 - 1


def iota(shape, dim):
    return lax.broadcasted_iota(jnp.int32, shape, dim)


def dot(a, b):
    return jnp.dot(a, b, preferred_element_type=F32)


def dot_nt(a, b):
    return lax.dot_general(a, b, (((1,), (1,)), ((), ())), preferred_element_type=F32)


def parts3(value):
    high = value.astype(BF16)
    rest = value - high.astype(F32)
    mid = rest.astype(BF16)
    low = (rest - mid.astype(F32)).astype(BF16)
    return jnp.concatenate([high, mid, low], axis=0)


def kernel(
    sizes, vel_ref, pos_ref, force_ref, flag_ref, tile_ref, grid_ref, out_ref,
    send, recv, along, across, picks, gather_t, scaled, pieces, low_grid, local_u, ret_send, ret_recv,
    face_y_send, face_z_send, face_x, face_y, face_z,
    send_sem, recv_sem, rsend_sem, rrecv_sem, hsend_sem, hrecv_sem,
):
    names = ("gx", "gy", "gz")
    me = [lax.axis_index(name) for name in names]
    around = [
        {d: lax.rem(at + (d + size), size) for d in (-1, 0, 1)} for at, size in zip(me, sizes)
    ]

    def near(offset):
        return tuple(around[i][offset[i]] for i in range(3))

    barrier = pltpu.get_barrier_semaphore()
    for n in range(NEAR):
        pl.semaphore_signal(barrier, inc=1, device_id=near(static_offsets(n)), device_id_type=MESH)

    rows = CHUNKS * CAP
    flags = flag_ref[...].astype(F32)
    before = (iota((64, 64), 0) <= iota((64, 64), 1)).astype(F32).astype(BF16)
    ranks = dot(flags.astype(BF16), before) - 1.0
    value = jnp.where(flags > 0.5, ranks, -1.0)
    value = jnp.concatenate([value, value, value], axis=1)
    row_chunk = iota((rows, 27), 0) // CAP
    chooser = (code_of(row_chunk) == iota((rows, 27), 1)).astype(F32).astype(BF16)
    row_value = dot(chooser, value.astype(BF16))
    own_value = (iota((rows, 192), 1) % 64 - (iota((rows, 192), 0) // CAP - NEAR) * CAP).astype(F32)
    row_value = jnp.where(iota((rows, 192), 0) >= NEAR * CAP, own_value, row_value)
    chosen = jnp.where(row_value == (iota((rows, 192), 0) % CAP).astype(F32), 1.0, 0.0)
    pick = chosen.astype(BF16)
    for f in range(6):
        source = pos_ref[f] if f < 3 else force_ref[f - 3]
        got = dot(pick, parts3(source)).reshape(CHUNKS, CAP, 256)
        send[:, f * CAP : (f + 1) * CAP, :] = got[:NEAR]
        recv[NEAR:, f * CAP : (f + 1) * CAP, :] = got[NEAR:]
    ids = (tile_ref[...].reshape(27 * CAP, 64) + 1).astype(F32).astype(BF16)
    all_ids = dot_nt(pick[:, :64], ids)
    same = code_of(iota((rows, 27 * CAP), 0) // CAP) == iota((rows, 27 * CAP), 1) // CAP
    all_ids = jnp.where(same, all_ids, 0.0).astype(BF16)
    spread_ids = (iota((27 * CAP, 256), 0) % CAP == iota((27 * CAP, 256), 1) % CAP).astype(F32).astype(BF16)
    wide = dot(all_ids, spread_ids)
    wide = jnp.where(iota((rows, 256), 0) % CAP == iota((rows, 256), 1) // CAP, wide, 0.0)
    id_rows = jnp.sum(wide.reshape(CHUNKS, CAP, 256), axis=1, keepdims=True) - 1.0
    id_rows = jnp.broadcast_to(id_rows, (CHUNKS, 8, 256))
    send[:, 96:104, :] = id_rows[:NEAR]
    recv[NEAR:, 96:104, :] = id_rows[NEAR:]

    last_row = (iota((CAP, 256), 1) == iota((CAP, 256), 0) * CAP + 15).astype(F32)
    first_row = (iota((CAP, 256), 1) == iota((CAP, 256), 0) * CAP).astype(F32)
    z_low, z_high = [], []
    for k in range(3):
        plane = vel_ref[:, k].reshape(256, 128)
        turned = plane.T
        z_low.append(turned[0:1])
        z_high.append(turned[127:128])
        face_y_send[0, k] = jnp.dot(last_row, plane, precision=lax.Precision.HIGHEST, preferred_element_type=F32)
        face_y_send[1, k] = jnp.dot(first_row, plane, precision=lax.Precision.HIGHEST, preferred_element_type=F32)
    pad = [jnp.zeros((5, 256), F32)]
    face_z_send[0] = jnp.concatenate(z_high + pad, axis=0)
    face_z_send[1] = jnp.concatenate(z_low + pad, axis=0)

    def halo(index):
        axis, side = divmod(index, 2)
        offset = [0, 0, 0]
        offset[axis] = 1 - 2 * side
        source = (vel_ref.at[15 if side == 0 else 0], face_y_send.at[side], face_z_send.at[side])[axis]
        target = (face_x.at[side], face_y.at[side], face_z.at[side])[axis]
        return pltpu.make_async_remote_copy(
            src_ref=source, dst_ref=target, send_sem=hsend_sem.at[index], recv_sem=hrecv_sem.at[index],
            device_id=near(offset), device_id_type=MESH,
        )

    def forward(n, device):
        return pltpu.make_async_remote_copy(
            src_ref=send.at[n], dst_ref=recv.at[n], send_sem=send_sem.at[n], recv_sem=recv_sem.at[n],
            device_id=device, device_id_type=MESH,
        )

    def back(n, device):
        return pltpu.make_async_remote_copy(
            src_ref=ret_send.at[n], dst_ref=ret_recv.at[n], send_sem=rsend_sem.at[n], recv_sem=rrecv_sem.at[n],
            device_id=device, device_id_type=MESH,
        )

    pl.semaphore_wait(barrier, NEAR)
    halos = [halo(i) for i in range(6)]
    for copy in halos:
        copy.start()
    for n in range(NEAR):
        forward(n, near(static_offsets(n))).start()

    gather_t[...] = jnp.concatenate([chosen[:, :128], jnp.zeros((32, 128), F32)], axis=0).T.astype(BF16)

    tile_y = iota((256, 128), 0) % CAP
    lane = iota((256, 128), 1)
    for k in range(3):
        plane = vel_ref[:, k].reshape(256, 128)
        near_y = jnp.where(tile_y == 0, 0.0, pltpu.roll(plane, 1, 0)) + jnp.where(
            tile_y == 15, 0.0, pltpu.roll(plane, 255, 0)
        )
        near_z = jnp.where(lane == 0, 0.0, pltpu.roll(plane, 1, 1)) + jnp.where(
            lane == 127, 0.0, pltpu.roll(plane, 127, 1)
        )
        none = jnp.zeros((CAP, 128), F32)
        near_x = jnp.concatenate([none, plane[:240]], axis=0) + jnp.concatenate([plane[16:], none], axis=0)
        total = plane + 0.1 * (near_x + near_y + near_z - 6.0 * plane)
        grid_ref[:, k] = total.reshape(16, 16, 128)

    def spread(chunk):
        off_x, off_y, off_z = offsets_of(chunk)
        ids = recv[chunk, 96:97, :]
        column = jnp.broadcast_to(ids, (128, 256)).T
        tile_x = jnp.floor(column * 0.0625)
        tile_y = column - 16.0 * tile_x
        placing = jnp.where(iota((256, 256), 0).astype(F32) == ids, 1.0, 0.0).astype(BF16)
        half = iota((256, 128), 1).astype(F32)
        picks[chunk, :, 0:128] = jnp.where(column == half, 1.0, 0.0).astype(BF16)
        picks[chunk, :, 128:256] = jnp.where(column == half + 128.0, 1.0, 0.0).astype(BF16)
        x = (recv[chunk, 0:16, :] - (off_x * 16).astype(F32)) * ROOT
        y = (recv[chunk, 16:32, :] - (off_y * 16).astype(F32)) * ROOT
        z = (recv[chunk, 32:48, :] - (off_z * 128).astype(F32)) * ROOT
        forces = [recv[chunk, 48 + 16 * k : 64 + 16 * k, :] for k in range(3)]
        cell = iota((128, 256), 0).astype(F32) * ROOT
        for r in range(CAP):
            part = slice(r * 16, r * 16 + 16)
            tx = tile_x[part] * ROOT
            ty = tile_y[part] * ROOT
            there = column[part]
            dx = jnp.concatenate([tx, tx], axis=1) - x[r : r + 1]
            dy = jnp.concatenate([ty, ty], axis=1) - y[r : r + 1]
            weight = jnp.exp2(-(dx * dx + dy * dy))
            weight = jnp.where(jnp.concatenate([there, there], axis=1) >= 0.0, weight, 0.0)
            across[chunk, r] = weight
            for k in range(3):
                scaled[r, 16 * k : 16 * k + 16, :] = (forces[k][r : r + 1] * weight).astype(BF16)
            dz = cell - z[r : r + 1]
            line = jnp.exp2(-(dz * dz)).astype(BF16)
            along[chunk, r] = line
            piece = dot_nt(scaled[r], line)
            for k in range(3):
                pieces[part, 128 * k : 128 * k + 128] = piece[16 * k : 16 * k + 16].astype(BF16)
        added = dot(placing, pieces[...])
        for k in range(3):
            grid_ref[:, k] += added[:, 128 * k : 128 * k + 128].reshape(16, 16, 128)

    @pl.loop(NEAR, CHUNKS)
    def _(chunk):
        spread(chunk)

    for copy in halos:
        copy.wait()
    at_row0 = (iota((256, CAP), 0) == iota((256, CAP), 1) * CAP).astype(F32)
    at_row15 = (iota((256, CAP), 0) == iota((256, CAP), 1) * CAP + 15).astype(F32)
    for k in range(3):
        grid_ref[0, k] += 0.1 * face_x[0, k]
        grid_ref[15, k] += 0.1 * face_x[1, k]
        extra = jnp.dot(at_row0, face_y[0, k], precision=lax.Precision.HIGHEST, preferred_element_type=F32)
        extra += jnp.dot(at_row15, face_y[1, k], precision=lax.Precision.HIGHEST, preferred_element_type=F32)
        low = jnp.broadcast_to(face_z[0, k : k + 1, :], (128, 256)).T
        high = jnp.broadcast_to(face_z[1, k : k + 1, :], (128, 256)).T
        extra += jnp.where(lane == 0, low, 0.0) + jnp.where(lane == 127, high, 0.0)
        grid_ref[:, k] += 0.1 * extra.reshape(16, 16, 128)

    beside = near((1, 0, 0))

    @pl.loop(0, NEAR)
    def _(chunk):
        forward(chunk, beside).wait_recv()
        spread(chunk)

    for k in range(3):
        low_grid[:, 128 * k : 128 * k + 128] = grid_ref[:, k].reshape(256, 128).astype(BF16)

    def sample(chunk, result):
        u = dot(picks[chunk], low_grid[...]).astype(BF16)
        for k in range(3):
            local_u[:, 16 * k : 16 * k + 16, :] = u[:, 128 * k : 128 * k + 128].reshape(16, 16, 128)
        for r in range(CAP):
            got = dot(local_u[r], along[chunk, r])
            weight = across[chunk, r]
            for k in range(3):
                result[k, r : r + 1, :] = jnp.sum(got[16 * k : 16 * k + 16] * weight, axis=0, keepdims=True)

    def origin(chunk):
        offset = offsets_of(chunk)
        return tuple(lax.rem(me[i] - offset[i] + sizes[i], sizes[i]) for i in range(3))

    @pl.loop(0, NEAR)
    def _(chunk):
        sample(chunk, ret_send.at[chunk])
        back(chunk, origin(chunk)).start()

    @pl.loop(NEAR, CHUNKS)
    def _(chunk):
        sample(chunk, ret_recv.at[chunk])

    @pl.loop(0, NEAR)
    def _(chunk):
        forward(chunk, beside).wait_send()
        back(chunk, beside).wait()

    gather = gather_t[0:64, 0:rows]
    for k in range(3):
        terms = ret_recv[:, k].reshape(rows, 256)
        high = terms.astype(BF16)
        low = (terms - high.astype(F32)).astype(BF16)
        out_ref[k] = dot(gather, high) + dot(gather, low)


def body(sizes, velocity, marker_pos, marker_force, intersect, tiles):
    vmem = pl.BlockSpec(memory_space=pltpu.VMEM)
    dma = pltpu.SemaphoreType.DMA
    grid, markers = pl.pallas_call(
        functools.partial(kernel, sizes),
        out_shape=(
            jax.ShapeDtypeStruct((16, 3, 16, 128), F32),
            jax.ShapeDtypeStruct((3, 64, 256), F32),
        ),
        in_specs=[vmem] * 5,
        out_specs=(vmem, vmem),
        scratch_shapes=[
            pltpu.VMEM((NEAR, 104, 256), F32),
            pltpu.VMEM((CHUNKS, 104, 256), F32),
            pltpu.VMEM((CHUNKS, CAP, 128, 256), BF16),
            pltpu.VMEM((CHUNKS, CAP, CAP, 256), F32),
            pltpu.VMEM((CHUNKS, 256, 256), BF16),
            pltpu.VMEM((128, 512), BF16),
            pltpu.VMEM((CAP, 48, 256), BF16),
            pltpu.VMEM((256, 384), BF16),
            pltpu.VMEM((256, 384), BF16),
            pltpu.VMEM((CAP, 48, 128), BF16),
            pltpu.VMEM((NEAR, 3, CAP, 256), F32),
            pltpu.VMEM((CHUNKS, 3, CAP, 256), F32),
            pltpu.VMEM((2, 3, CAP, 128), F32),
            pltpu.VMEM((2, 8, 256), F32),
            pltpu.VMEM((2, 3, CAP, 128), F32),
            pltpu.VMEM((2, 3, CAP, 128), F32),
            pltpu.VMEM((2, 8, 256), F32),
            dma((NEAR,)),
            dma((NEAR,)),
            dma((NEAR,)),
            dma((NEAR,)),
            dma((6,)),
            dma((6,)),
        ],
        compiler_params=pltpu.CompilerParams(
            collective_id=0, has_side_effects=True, vmem_limit_bytes=67043328
        ),
    )(
        jnp.transpose(velocity, (0, 2, 1, 3)),
        jnp.transpose(marker_pos, (1, 0, 2)),
        jnp.transpose(marker_force, (1, 0, 2)),
        intersect.T,
        jnp.transpose(tiles, (1, 2, 0)),
    )
    return jnp.transpose(grid, (0, 2, 1, 3)), jnp.transpose(markers, (1, 0, 2))


def solution(mesh):
    sizes = tuple(mesh.shape[name] for name in ("gx", "gy", "gz"))
    placed = (
        P("gx", "gy", None, "gz"),
        P(("gx", "gy", "gz"), None, None),
        P(("gx", "gy", "gz"), None, None),
        P(("gx", "gy", "gz"), None),
        P(("gx", "gy", "gz"), None, None),
    )
    return jax.shard_map(
        functools.partial(body, sizes),
        mesh=mesh,
        in_specs=placed,
        out_specs=(P("gx", "gy", None, "gz"), P(("gx", "gy", "gz"), None, None)),
        check_vma=False,
    )
```

time: 301 us -> 69.9 us (0.23)
  the two profiles are of different devices: /device:TPU:54 before, /device:TPU:6 now
where the time goes in v1:
time: 69.9 us; the launch traced here: 69.8 us
  Pallas kernels  66.7 us (95%)
  local copies, waits for them, and re-layouts  2.49 us (4%)
    pallas_call x1, Pallas kernels, body(): pl.pallas_call(functools.partial(kernel, sizes), out_shape=(jax.ShapeDtyp...  66.7 us
    unnamed x4, local copies, waits for them, and re-layouts  2.49 us

profile of v1, /device:TPU:6, one launch (start us, length us, event | category | flops | bytes accessed | tf_op | source)
XLA Modules:
  0.0 69.8 jit_solution(13147326329979407483)
XLA Ops:
  0.6 66.7 %shard_map.68 = (f32[16,3,16,128]{3,2,1,0:T(8,128)}, f32[3,64,256]{2,1,0:T(8,128)}) custom-call(f32[16,3,16,128]{3,2,1,0:T(8,128)} %bitcast.8, f32[3,64,256]{2,1,0:T(8,128)} %bitcast.11, f32[3,64,256]{2,1,0:T(8,128)} %bitcast.12, s32[27,64]{1,0:T(8,128)} %bitcast.13, s32[27,16,64]{2,1,0:T(8,128)} %bitcast.9), custom_call_target="tpu_custom_call" | custom-call | tf_op jit(solution)/shard_map/pallas_call | solution.py:269
  67.3 0.0 copy-start
  67.3 1.8 %copy.9 = f32[16,16,3,128]{3,1,2,0:T(8,128)} copy(f32[16,16,3,128]{3,1,2,0:T(8,128)} %bitcast.7) | data formatting | bytes 786432
  69.1 0.0 copy-done
  69.1 0.7 copy.10
Async XLA Ops:
  67.3 1.8 %copy-start = (f32[3,64,256]{2,1,0:T(8,128)S(1)}, f32[3,64,256]{2,1,0:T(8,128)}, u32[]{:S(2)}) copy-start(f32[3,64,256]{2,1,0:T(8,128)} %get-tuple-element.5) | copy-start | bytes 589828

commit v2 on v1

--- a/solution.py
+++ b/solution.py
@@ -11,15 +11,34 @@
 CAP = 16
 NEAR = 26
 CHUNKS = 30
-STEP = 5
 LOG2E = 1.4426950408889634
 ROOT = (0.5 * LOG2E) ** 0.5
+HALF = -0.5 * LOG2E
 F32 = jnp.float32
 BF16 = jnp.bfloat16
 
 
+FACES = [(1, 0, 0), (0, 0, 1), (0, 1, 0), (-1, 0, 0), (0, 0, -1), (0, -1, 0)]
+EDGES = [
+    (1, 0, 1), (0, 1, -1), (-1, 1, 0), (0, -1, 1), (-1, 0, -1), (1, -1, 0),
+    (1, 1, 0), (0, -1, -1), (-1, 0, 1), (0, 1, 1), (1, 0, -1), (-1, -1, 0),
+]
+CORNERS = [
+    (1, 1, 1), (-1, -1, -1), (1, -1, 1), (-1, 1, -1), (-1, 1, 1), (1, -1, -1), (1, 1, -1), (-1, -1, 1),
+]
+ORDER = FACES + EDGES + CORNERS + [(0, 0, 0)] * 4
+WORDS = [
+    sum((13 + 9 * x + 3 * y + z) << (5 * i) for i, (x, y, z) in enumerate(ORDER[6 * w : 6 * w + 6]))
+    for w in range(5)
+]
+
+
 def code_of(chunk):
-    return (13 + STEP * jnp.minimum(chunk + 1, 27)) % 27
+    word = jnp.where(chunk < 6, WORDS[0], WORDS[1])
+    word = jnp.where(chunk < 12, word, WORDS[2])
+    word = jnp.where(chunk < 18, word, WORDS[3])
+    word = jnp.where(chunk < 24, word, WORDS[4])
+    return lax.shift_right_logical(word, 5 * (chunk % 6)) % 32
 
 
 def offsets_of(chunk):
@@ -27,11 +46,6 @@
     return code // 9 - 1, code // 3 % 3 - 1, code % 3 - 1
 
 
-def static_offsets(chunk):
-    code = (13 + STEP * min(chunk + 1, 27)) % 27
-    return code // 9 - 1, code // 3 % 3 - 1, code % 3 - 1
-
-
 def iota(shape, dim):
     return lax.broadcasted_iota(jnp.int32, shape, dim)
 
@@ -42,6 +56,27 @@
 
 def dot_nt(a, b):
     return lax.dot_general(a, b, (((1,), (1,)), ((), ())), preferred_element_type=F32)
+
+
+def onehot(index, ids):
+    return jnp.where(index.astype(F32) == ids, 1.0, 0.0).astype(BF16)
+
+
+def merged(values):
+    row = iota((8, 256), 0)
+    for width in (4, 2, 1):
+        first = row % (2 * width) < width
+        if width == 4:
+            values = [
+                jnp.where(first, a, b) + pltpu.roll(jnp.where(first, b, a), 4, 0)
+                for a, b in zip(values[:4], values[4:])
+            ]
+        else:
+            values = [
+                jnp.where(first, a, b) + jnp.where(first, pltpu.roll(a, 8 - width, 0), pltpu.roll(b, width, 0))
+                for a, b in zip(values[:width], values[width:])
+            ]
+    return values[0]
 
 
 def parts3(value):
@@ -54,9 +89,9 @@
 
 def kernel(
     sizes, vel_ref, pos_ref, force_ref, flag_ref, tile_ref, grid_ref, out_ref,
-    send, recv, along, across, picks, gather_t, scaled, pieces, low_grid, local_u, ret_send, ret_recv,
+    send, recv, send_ids, recv_ids, along, across, picks, gather_t, pieces, low_grid, local_u, ret_send, ret_recv,
     face_y_send, face_z_send, face_x, face_y, face_z,
-    send_sem, recv_sem, rsend_sem, rrecv_sem, hsend_sem, hrecv_sem,
+    round_sem, send_sem, recv_sem, isend_sem, irecv_sem, rsend_sem, rrecv_sem, hsend_sem, hrecv_sem,
 ):
     names = ("gx", "gy", "gz")
     me = [lax.axis_index(name) for name in names]
@@ -68,8 +103,8 @@
         return tuple(around[i][offset[i]] for i in range(3))
 
     barrier = pltpu.get_barrier_semaphore()
-    for n in range(NEAR):
-        pl.semaphore_signal(barrier, inc=1, device_id=near(static_offsets(n)), device_id_type=MESH)
+    for face in FACES:
+        pl.semaphore_signal(barrier, inc=1, device_id=near(face), device_id_type=MESH)
 
     rows = CHUNKS * CAP
     flags = flag_ref[...].astype(F32)
@@ -97,9 +132,8 @@
     wide = dot(all_ids, spread_ids)
     wide = jnp.where(iota((rows, 256), 0) % CAP == iota((rows, 256), 1) // CAP, wide, 0.0)
     id_rows = jnp.sum(wide.reshape(CHUNKS, CAP, 256), axis=1, keepdims=True) - 1.0
-    id_rows = jnp.broadcast_to(id_rows, (CHUNKS, 8, 256))
-    send[:, 96:104, :] = id_rows[:NEAR]
-    recv[NEAR:, 96:104, :] = id_rows[NEAR:]
+    send_ids[...] = id_rows[:NEAR]
+    recv_ids[NEAR:] = id_rows[NEAR:]
 
     last_row = (iota((CAP, 256), 1) == iota((CAP, 256), 0) * CAP + 15).astype(F32)
     first_row = (iota((CAP, 256), 1) == iota((CAP, 256), 0) * CAP).astype(F32)
@@ -132,18 +166,33 @@
             device_id=device, device_id_type=MESH,
         )
 
+    def forward_ids(n, device):
+        return pltpu.make_async_remote_copy(
+            src_ref=send_ids.at[n], dst_ref=recv_ids.at[n], send_sem=isend_sem.at[n], recv_sem=irecv_sem.at[n],
+            device_id=device, device_id_type=MESH,
+        )
+
+    def go(low, high):
+        for n in range(low, high):
+            forward_ids(n, near(ORDER[n])).start()
+            forward(n, near(ORDER[n])).start()
+
+    def tell(index):
+        for face in FACES:
+            pl.semaphore_signal(round_sem.at[index], inc=1, device_id=near(face), device_id_type=MESH)
+
     def back(n, device):
         return pltpu.make_async_remote_copy(
             src_ref=ret_send.at[n], dst_ref=ret_recv.at[n], send_sem=rsend_sem.at[n], recv_sem=rrecv_sem.at[n],
             device_id=device, device_id_type=MESH,
         )
 
-    pl.semaphore_wait(barrier, NEAR)
+    pl.semaphore_wait(barrier, 6)
+    tell(0)
     halos = [halo(i) for i in range(6)]
     for copy in halos:
         copy.start()
-    for n in range(NEAR):
-        forward(n, near(static_offsets(n))).start()
+    go(0, 6)
 
     gather_t[...] = jnp.concatenate([chosen[:, :128], jnp.zeros((32, 128), F32)], axis=0).T.astype(BF16)
 
@@ -159,24 +208,23 @@
         )
         none = jnp.zeros((CAP, 128), F32)
         near_x = jnp.concatenate([none, plane[:240]], axis=0) + jnp.concatenate([plane[16:], none], axis=0)
-        total = plane + 0.1 * (near_x + near_y + near_z - 6.0 * plane)
+        total = 0.1 * (near_x + near_y + near_z - 6.0 * plane)
         grid_ref[:, k] = total.reshape(16, 16, 128)
 
     def spread(chunk):
         off_x, off_y, off_z = offsets_of(chunk)
-        ids = recv[chunk, 96:97, :]
+        ids = recv_ids[chunk]
         column = jnp.broadcast_to(ids, (128, 256)).T
         tile_x = jnp.floor(column * 0.0625)
         tile_y = column - 16.0 * tile_x
-        placing = jnp.where(iota((256, 256), 0).astype(F32) == ids, 1.0, 0.0).astype(BF16)
-        half = iota((256, 128), 1).astype(F32)
-        picks[chunk, :, 0:128] = jnp.where(column == half, 1.0, 0.0).astype(BF16)
-        picks[chunk, :, 128:256] = jnp.where(column == half + 128.0, 1.0, 0.0).astype(BF16)
+        placing = onehot(iota((256, 256), 0), ids)
+        picks[chunk, 0] = onehot(iota((256, 128), 1), column)
+        picks[chunk, 1] = onehot(iota((256, 128), 1) + 128, column)
         x = (recv[chunk, 0:16, :] - (off_x * 16).astype(F32)) * ROOT
         y = (recv[chunk, 16:32, :] - (off_y * 16).astype(F32)) * ROOT
-        z = (recv[chunk, 32:48, :] - (off_z * 128).astype(F32)) * ROOT
+        z = recv[chunk, 32:48, :] - (off_z * 128).astype(F32) - 64.0
         forces = [recv[chunk, 48 + 16 * k : 64 + 16 * k, :] for k in range(3)]
-        cell = iota((128, 256), 0).astype(F32) * ROOT
+        step = iota((8, 256), 0).astype(F32)
         for r in range(CAP):
             part = slice(r * 16, r * 16 + 16)
             tx = tile_x[part] * ROOT
@@ -187,21 +235,46 @@
             weight = jnp.exp2(-(dx * dx + dy * dy))
             weight = jnp.where(jnp.concatenate([there, there], axis=1) >= 0.0, weight, 0.0)
             across[chunk, r] = weight
+            scaled = jnp.concatenate([(forces[k][r : r + 1] * weight).astype(BF16) for k in range(3)], axis=0)
+            dz = step - z[r : r + 1]
+            lean = dz * (16.0 * HALF)
+            start = dz * dz * HALF
+            powers = {8: start}
+            up, down = lean + 64.0 * HALF, 64.0 * HALF - lean
+            at = start
+            for g in range(9, 16):
+                at = at + up
+                powers[g] = at
+                up = up + 128.0 * HALF
+            at = start
+            for g in range(7, -1, -1):
+                at = at + down
+                powers[g] = at
+                down = down + 128.0 * HALF
+            line = jnp.concatenate([jnp.exp2(powers[g]) for g in range(16)], axis=0).astype(BF16)
+            along[chunk, r, 0] = line[:, :128]
+            along[chunk, r, 1] = line[:, 128:]
+            piece = dot_nt(scaled, line).astype(BF16)
             for k in range(3):
-                scaled[r, 16 * k : 16 * k + 16, :] = (forces[k][r : r + 1] * weight).astype(BF16)
-            dz = cell - z[r : r + 1]
-            line = jnp.exp2(-(dz * dz)).astype(BF16)
-            along[chunk, r] = line
-            piece = dot_nt(scaled[r], line)
-            for k in range(3):
-                pieces[part, 128 * k : 128 * k + 128] = piece[16 * k : 16 * k + 16].astype(BF16)
-        added = dot(placing, pieces[...])
+                pieces[k, part, :] = piece[16 * k : 16 * k + 16]
+        added = dot(placing, jnp.concatenate([pieces[k] for k in range(3)], axis=1))
         for k in range(3):
             grid_ref[:, k] += added[:, 128 * k : 128 * k + 128].reshape(16, 16, 128)
 
-    @pl.loop(NEAR, CHUNKS)
+    @pl.loop(NEAR, NEAR + 2)
     def _(chunk):
         spread(chunk)
+
+    pl.semaphore_wait(round_sem.at[0], 6)
+    tell(1)
+    go(6, 18)
+
+    @pl.loop(NEAR + 2, CHUNKS)
+    def _(chunk):
+        spread(chunk)
+
+    pl.semaphore_wait(round_sem.at[1], 6)
+    go(18, NEAR)
 
     for copy in halos:
         copy.wait()
@@ -221,28 +294,37 @@
 
     @pl.loop(0, NEAR)
     def _(chunk):
+        forward_ids(chunk, beside).wait_recv()
         forward(chunk, beside).wait_recv()
         spread(chunk)
 
     for k in range(3):
-        low_grid[:, 128 * k : 128 * k + 128] = grid_ref[:, k].reshape(256, 128).astype(BF16)
+        low_grid[k] = (vel_ref[:, k] + grid_ref[:, k]).reshape(256, 128).astype(BF16)
 
     def sample(chunk, result):
-        u = dot(picks[chunk], low_grid[...]).astype(BF16)
+        pick_rows = jnp.concatenate([picks[chunk, 0], picks[chunk, 1]], axis=1)
+        u = dot(pick_rows, jnp.concatenate([low_grid[k] for k in range(3)], axis=1)).astype(BF16)
         for k in range(3):
             local_u[:, 16 * k : 16 * k + 16, :] = u[:, 128 * k : 128 * k + 128].reshape(16, 16, 128)
-        for r in range(CAP):
-            got = dot(local_u[r], along[chunk, r])
-            weight = across[chunk, r]
+        for half in range(2):
+            sums = [[], [], []]
+            for r in range(8 * half, 8 * half + 8):
+                line = jnp.concatenate([along[chunk, r, 0], along[chunk, r, 1]], axis=1)
+                got = dot(local_u[r], line)
+                weight = across[chunk, r]
+                for k in range(3):
+                    value = got[16 * k : 16 * k + 16] * weight
+                    sums[k].append(value[0:8] + value[8:16])
             for k in range(3):
-                result[k, r : r + 1, :] = jnp.sum(got[16 * k : 16 * k + 16] * weight, axis=0, keepdims=True)
+                result[k, 8 * half : 8 * half + 8, :] = merged(sums[k])
 
     def origin(chunk):
         offset = offsets_of(chunk)
         return tuple(lax.rem(me[i] - offset[i] + sizes[i], sizes[i]) for i in range(3))
 
     @pl.loop(0, NEAR)
-    def _(chunk):
+    def _(turn):
+        chunk = NEAR - 1 - turn
         sample(chunk, ret_send.at[chunk])
         back(chunk, origin(chunk)).start()
 
@@ -252,6 +334,7 @@
 
     @pl.loop(0, NEAR)
     def _(chunk):
+        forward_ids(chunk, beside).wait_send()
         forward(chunk, beside).wait_send()
         back(chunk, beside).wait()
 
@@ -275,15 +358,16 @@
         in_specs=[vmem] * 5,
         out_specs=(vmem, vmem),
         scratch_shapes=[
-            pltpu.VMEM((NEAR, 104, 256), F32),
-            pltpu.VMEM((CHUNKS, 104, 256), F32),
-            pltpu.VMEM((CHUNKS, CAP, 128, 256), BF16),
+            pltpu.VMEM((NEAR, 96, 256), F32),
+            pltpu.VMEM((CHUNKS, 96, 256), F32),
+            pltpu.VMEM((NEAR, 1, 256), F32),
+            pltpu.VMEM((CHUNKS, 1, 256), F32),
+            pltpu.VMEM((CHUNKS, CAP, 2, 128, 128), BF16),
             pltpu.VMEM((CHUNKS, CAP, CAP, 256), F32),
-            pltpu.VMEM((CHUNKS, 256, 256), BF16),
+            pltpu.VMEM((CHUNKS, 2, 256, 128), BF16),
             pltpu.VMEM((128, 512), BF16),
-            pltpu.VMEM((CAP, 48, 256), BF16),
-            pltpu.VMEM((256, 384), BF16),
-            pltpu.VMEM((256, 384), BF16),
+            pltpu.VMEM((3, 256, 128), BF16),
+            pltpu.VMEM((3, 256, 128), BF16),
             pltpu.VMEM((CAP, 48, 128), BF16),
             pltpu.VMEM((NEAR, 3, CAP, 256), F32),
             pltpu.VMEM((CHUNKS, 3, CAP, 256), F32),
@@ -292,6 +376,9 @@
             pltpu.VMEM((2, 3, CAP, 128), F32),
             pltpu.VMEM((2, 3, CAP, 128), F32),
             pltpu.VMEM((2, 8, 256), F32),
+            pltpu.SemaphoreType.REGULAR((2,)),
+            dma((NEAR,)),
+            dma((NEAR,)),
             dma((NEAR,)),
             dma((NEAR,)),
             dma((NEAR,)),
@@ -309,7 +396,7 @@
         intersect.T,
         jnp.transpose(tiles, (1, 2, 0)),
     )
-    return jnp.transpose(grid, (0, 2, 1, 3)), jnp.transpose(markers, (1, 0, 2))
+    return velocity + jnp.transpose(grid, (0, 2, 1, 3)), jnp.transpose(markers, (1, 0, 2))
 
 
 def solution(mesh):

time: 69.9 us -> 59.7 us (0.85)
  the two profiles are of different devices: /device:TPU:6 before, /device:TPU:1 now
where the time goes in v2:
time: 59.7 us; the launch traced here: 59.6 us
  Pallas kernels  56.3 us (94%)
  other arithmetic  1.95 us (3%)
  local copies, waits for them, and re-layouts  0.68 us (1%)
  between operations  0.65 us (1%)
    pallas_call x1, Pallas kernels, body(): pl.pallas_call(functools.partial(kernel, sizes), out_shape=(jax.ShapeDtyp...  56.3 us
    add x1, other arithmetic, body(): velocity + jnp.transpose(grid, (0, 2, 1, 3))  1.95 us

profile of v2, /device:TPU:1, one launch (start us, length us, event | category | flops | bytes accessed | tf_op | source)
XLA Modules:
  0.0 59.6 jit_solution(1384686393666638787)
XLA Ops:
  0.6 56.3 %shard_map.68 = (f32[16,3,16,128]{3,2,1,0:T(8,128)}, f32[3,64,256]{2,1,0:T(8,128)}) custom-call(f32[16,3,16,128]{3,2,1,0:T(8,128)} %bitcast.8, f32[3,64,256]{2,1,0:T(8,128)} %bitcast.11, f32[3,64,256]{2,1,0:T(8,128)} %bitcast.12, s32[27,64]{1,0:T(8,128)} %bitcast.13, s32[27,16,64]{2,1,0:T(8,128)} %bitcast.9), custom_call_target="tpu_custom_call" | custom-call | tf_op jit(solution)/shard_map/pallas_call | solution.py:352
  57.0 0.0 copy-start
  57.0 1.9 %bitcast_add_fusion = f32[16,16,3,128]{3,1,2,0:T(8,128)} fusion(f32[16,16,3,128]{3,1,2,0:T(8,128)} %param.5, f32[16,3,16,128]{3,2,1,0:T(8,128)} %get-tuple-element.4), kind=kLoop, calls=%fused_computation | loop fusion | flops 98304 | bytes 1179648 | tf_op jit(solution)/shard_map/add | solution.py:399
  58.9 0.0 copy-done
  58.9 0.7 %copy.8 = f32[64,3,256]{2,0,1:T(8,128)} copy(f32[64,3,256]{2,0,1:T(8,128)S(1)} %bitcast.10) | data formatting | bytes 393216
Async XLA Ops:
  57.0 2.0 %copy-start = (f32[3,64,256]{2,1,0:T(8,128)S(1)}, f32[3,64,256]{2,1,0:T(8,128)}, u32[]{:S(2)}) copy-start(f32[3,64,256]{2,1,0:T(8,128)} %get-tuple-element.5) | copy-start | bytes 589828

commit v3 on v2

--- a/solution.py
+++ b/solution.py
@@ -88,7 +88,8 @@
 
 
 def kernel(
-    sizes, vel_ref, pos_ref, force_ref, flag_ref, tile_ref, grid_ref, out_ref,
+    sizes, vel_in, pos_in, force_in, flag_in, tile_in, grid_ref, out_ref,
+    vel_ref, pos_ref, force_ref, flag_ref, tile_ref, in_sem, split,
     send, recv, send_ids, recv_ids, along, across, picks, gather_t, pieces, low_grid, local_u, ret_send, ret_recv,
     face_y_send, face_z_send, face_x, face_y, face_z,
     round_sem, send_sem, recv_sem, isend_sem, irecv_sem, rsend_sem, rrecv_sem, hsend_sem, hrecv_sem,
@@ -106,35 +107,86 @@
     for face in FACES:
         pl.semaphore_signal(barrier, inc=1, device_id=near(face), device_id_type=MESH)
 
-    rows = CHUNKS * CAP
+    loads = [
+        pltpu.make_async_copy(source, target, in_sem.at[i])
+        for i, (source, target) in enumerate(
+            [(flag_in, flag_ref), (pos_in, pos_ref), (force_in, force_ref), (vel_in, vel_ref), (tile_in, tile_ref)]
+        )
+    ]
+    for copy in loads:
+        copy.start()
+
+    def halo(index):
+        axis, side = divmod(index, 2)
+        offset = [0, 0, 0]
+        offset[axis] = 1 - 2 * side
+        source = (vel_ref.at[15 if side == 0 else 0], face_y_send.at[side], face_z_send.at[side])[axis]
+        target = (face_x.at[side], face_y.at[side], face_z.at[side])[axis]
+        return pltpu.make_async_remote_copy(
+            src_ref=source, dst_ref=target, send_sem=hsend_sem.at[index], recv_sem=hrecv_sem.at[index],
+            device_id=near(offset), device_id_type=MESH,
+        )
+
+    def forward(n, device):
+        return pltpu.make_async_remote_copy(
+            src_ref=send.at[n], dst_ref=recv.at[n], send_sem=send_sem.at[n], recv_sem=recv_sem.at[n],
+            device_id=device, device_id_type=MESH,
+        )
+
+    def forward_ids(n, device):
+        return pltpu.make_async_remote_copy(
+            src_ref=send_ids.at[n], dst_ref=recv_ids.at[n], send_sem=isend_sem.at[n], recv_sem=irecv_sem.at[n],
+            device_id=device, device_id_type=MESH,
+        )
+
+    def go(low, high):
+        for n in range(low, high):
+            forward(n, near(ORDER[n])).start()
+
+    def go_ids(low, high):
+        for n in range(low, high):
+            forward_ids(n, near(ORDER[n])).start()
+
+    def tell(index):
+        for face in FACES:
+            pl.semaphore_signal(round_sem.at[index], inc=1, device_id=near(face), device_id_type=MESH)
+
+    def back(n, device):
+        return pltpu.make_async_remote_copy(
+            src_ref=ret_send.at[n], dst_ref=ret_recv.at[n], send_sem=rsend_sem.at[n], recv_sem=rrecv_sem.at[n],
+            device_id=device, device_id_type=MESH,
+        )
+
+    loads[0].wait()
     flags = flag_ref[...].astype(F32)
     before = (iota((64, 64), 0) <= iota((64, 64), 1)).astype(F32).astype(BF16)
     ranks = dot(flags.astype(BF16), before) - 1.0
     value = jnp.where(flags > 0.5, ranks, -1.0)
-    value = jnp.concatenate([value, value, value], axis=1)
-    row_chunk = iota((rows, 27), 0) // CAP
-    chooser = (code_of(row_chunk) == iota((rows, 27), 1)).astype(F32).astype(BF16)
-    row_value = dot(chooser, value.astype(BF16))
-    own_value = (iota((rows, 192), 1) % 64 - (iota((rows, 192), 0) // CAP - NEAR) * CAP).astype(F32)
-    row_value = jnp.where(iota((rows, 192), 0) >= NEAR * CAP, own_value, row_value)
-    chosen = jnp.where(row_value == (iota((rows, 192), 0) % CAP).astype(F32), 1.0, 0.0)
-    pick = chosen.astype(BF16)
+    value = jnp.concatenate([value, value, value], axis=1).astype(BF16)
+    lanes27 = iota((CAP, 27), 1)
+
+    def code_rows(low, high):
+        return jnp.concatenate(
+            [jnp.where(lanes27 == 13 + 9 * x + 3 * y + z, 1.0, 0.0) for x, y, z in ORDER[low:high]], axis=0
+        ).astype(BF16)
+
+    def slot_rows(low, high):
+        rows = (high - low) * CAP
+        slot = (iota((rows, 192), 0) & 15).astype(F32)
+        return jnp.where(dot(code_rows(low, high), value) == slot, 1.0, 0.0)
+
+    face_pick = slot_rows(0, 6).astype(BF16)
+    loads[1].wait()
+    loads[2].wait()
     for f in range(6):
-        source = pos_ref[f] if f < 3 else force_ref[f - 3]
-        got = dot(pick, parts3(source)).reshape(CHUNKS, CAP, 256)
-        send[:, f * CAP : (f + 1) * CAP, :] = got[:NEAR]
-        recv[NEAR:, f * CAP : (f + 1) * CAP, :] = got[NEAR:]
-    ids = (tile_ref[...].reshape(27 * CAP, 64) + 1).astype(F32).astype(BF16)
-    all_ids = dot_nt(pick[:, :64], ids)
-    same = code_of(iota((rows, 27 * CAP), 0) // CAP) == iota((rows, 27 * CAP), 1) // CAP
-    all_ids = jnp.where(same, all_ids, 0.0).astype(BF16)
-    spread_ids = (iota((27 * CAP, 256), 0) % CAP == iota((27 * CAP, 256), 1) % CAP).astype(F32).astype(BF16)
-    wide = dot(all_ids, spread_ids)
-    wide = jnp.where(iota((rows, 256), 0) % CAP == iota((rows, 256), 1) // CAP, wide, 0.0)
-    id_rows = jnp.sum(wide.reshape(CHUNKS, CAP, 256), axis=1, keepdims=True) - 1.0
-    send_ids[...] = id_rows[:NEAR]
-    recv_ids[NEAR:] = id_rows[NEAR:]
-
+        split[f] = parts3(pos_ref[f] if f < 3 else force_ref[f - 3])
+        send[0:6, f * CAP : (f + 1) * CAP, :] = dot(face_pick, split[f]).reshape(6, CAP, 256)
+
+    pl.semaphore_wait(barrier, 6)
+    tell(0)
+    go(0, 6)
+
+    loads[3].wait()
     last_row = (iota((CAP, 256), 1) == iota((CAP, 256), 0) * CAP + 15).astype(F32)
     first_row = (iota((CAP, 256), 1) == iota((CAP, 256), 0) * CAP).astype(F32)
     z_low, z_high = [], []
@@ -149,52 +201,43 @@
     face_z_send[0] = jnp.concatenate(z_high + pad, axis=0)
     face_z_send[1] = jnp.concatenate(z_low + pad, axis=0)
 
-    def halo(index):
-        axis, side = divmod(index, 2)
-        offset = [0, 0, 0]
-        offset[axis] = 1 - 2 * side
-        source = (vel_ref.at[15 if side == 0 else 0], face_y_send.at[side], face_z_send.at[side])[axis]
-        target = (face_x.at[side], face_y.at[side], face_z.at[side])[axis]
-        return pltpu.make_async_remote_copy(
-            src_ref=source, dst_ref=target, send_sem=hsend_sem.at[index], recv_sem=hrecv_sem.at[index],
-            device_id=near(offset), device_id_type=MESH,
-        )
-
-    def forward(n, device):
-        return pltpu.make_async_remote_copy(
-            src_ref=send.at[n], dst_ref=recv.at[n], send_sem=send_sem.at[n], recv_sem=recv_sem.at[n],
-            device_id=device, device_id_type=MESH,
-        )
-
-    def forward_ids(n, device):
-        return pltpu.make_async_remote_copy(
-            src_ref=send_ids.at[n], dst_ref=recv_ids.at[n], send_sem=isend_sem.at[n], recv_sem=irecv_sem.at[n],
-            device_id=device, device_id_type=MESH,
-        )
-
-    def go(low, high):
-        for n in range(low, high):
-            forward_ids(n, near(ORDER[n])).start()
-            forward(n, near(ORDER[n])).start()
-
-    def tell(index):
-        for face in FACES:
-            pl.semaphore_signal(round_sem.at[index], inc=1, device_id=near(face), device_id_type=MESH)
-
-    def back(n, device):
-        return pltpu.make_async_remote_copy(
-            src_ref=ret_send.at[n], dst_ref=ret_recv.at[n], send_sem=rsend_sem.at[n], recv_sem=rrecv_sem.at[n],
-            device_id=device, device_id_type=MESH,
-        )
-
-    pl.semaphore_wait(barrier, 6)
-    tell(0)
+    rest = slot_rows(6, NEAR)
+    rest_pick = rest.astype(BF16)
+    own_rows = jnp.where((iota((64, 192), 1) & 63) == iota((64, 192), 0), 1.0, 0.0)
+    own_pick = own_rows.astype(BF16)
+    for f in range(6):
+        got = dot(jnp.concatenate([rest_pick, own_pick], axis=0), split[f]).reshape(CHUNKS - 6, CAP, 256)
+        send[6:NEAR, f * CAP : (f + 1) * CAP, :] = got[: NEAR - 6]
+        recv[NEAR:, f * CAP : (f + 1) * CAP, :] = got[NEAR - 6 :]
     halos = [halo(i) for i in range(6)]
     for copy in halos:
         copy.start()
-    go(0, 6)
-
-    gather_t[...] = jnp.concatenate([chosen[:, :128], jnp.zeros((32, 128), F32)], axis=0).T.astype(BF16)
+    pl.semaphore_wait(round_sem.at[0], 6)
+    tell(1)
+
+    loads[4].wait()
+    rows = CHUNKS * CAP
+    pick = jnp.concatenate([face_pick, rest_pick, own_pick], axis=0)
+    ids = (tile_ref[...].reshape(27 * CAP, 64) + 1).astype(F32).astype(BF16)
+    all_ids = dot_nt(pick[:, :64], ids)
+    each = jnp.where(iota((27, 27 * CAP), 0) == lax.shift_right_logical(iota((27, 27 * CAP), 1), 4), 1.0, 0.0)
+    same = dot(code_rows(0, CHUNKS), each.astype(BF16))
+    all_ids = (all_ids * same).astype(BF16)
+    spread_ids = jnp.where((iota((27 * CAP, 256), 0) & 15) == (iota((27 * CAP, 256), 1) & 15), 1.0, 0.0).astype(BF16)
+    wide = dot(all_ids, spread_ids)
+    wide = jnp.where((iota((rows, 256), 0) & 15) == lax.shift_right_logical(iota((rows, 256), 1), 4), wide, 0.0)
+    id_rows = jnp.sum(wide.reshape(CHUNKS, CAP, 256), axis=1, keepdims=True) - 1.0
+    send_ids[...] = id_rows[:NEAR]
+    recv_ids[NEAR:] = id_rows[NEAR:]
+    go_ids(0, 18)
+    go(6, 18)
+    face_rows = slot_rows(0, 6)
+    gather_t[...] = jnp.concatenate(
+        [face_rows[:, :128], rest[:, :128], own_rows[:, :128], jnp.zeros((32, 128), F32)], axis=0
+    ).T.astype(BF16)
+    pl.semaphore_wait(round_sem.at[1], 6)
+    go_ids(18, NEAR)
+    go(18, NEAR)
 
     tile_y = iota((256, 128), 0) % CAP
     lane = iota((256, 128), 1)
@@ -208,10 +251,10 @@
         )
         none = jnp.zeros((CAP, 128), F32)
         near_x = jnp.concatenate([none, plane[:240]], axis=0) + jnp.concatenate([plane[16:], none], axis=0)
-        total = 0.1 * (near_x + near_y + near_z - 6.0 * plane)
+        total = plane + 0.1 * (near_x + near_y + near_z - 6.0 * plane)
         grid_ref[:, k] = total.reshape(16, 16, 128)
 
-    def spread(chunk):
+    def spread(chunk, slot):
         off_x, off_y, off_z = offsets_of(chunk)
         ids = recv_ids[chunk]
         column = jnp.broadcast_to(ids, (128, 256)).T
@@ -256,25 +299,18 @@
             along[chunk, r, 1] = line[:, 128:]
             piece = dot_nt(scaled, line).astype(BF16)
             for k in range(3):
-                pieces[k, part, :] = piece[16 * k : 16 * k + 16]
-        added = dot(placing, jnp.concatenate([pieces[k] for k in range(3)], axis=1))
+                pieces[slot, k, part, :] = piece[16 * k : 16 * k + 16]
+        added = dot(placing, jnp.concatenate([pieces[slot, k] for k in range(3)], axis=1))
         for k in range(3):
             grid_ref[:, k] += added[:, 128 * k : 128 * k + 128].reshape(16, 16, 128)
 
-    @pl.loop(NEAR, NEAR + 2)
+    def spread_pair(chunk):
+        spread(chunk, 0)
+        spread(chunk + 1, 1)
+
+    @pl.loop(NEAR, CHUNKS, step=2)
     def _(chunk):
-        spread(chunk)
-
-    pl.semaphore_wait(round_sem.at[0], 6)
-    tell(1)
-    go(6, 18)
-
-    @pl.loop(NEAR + 2, CHUNKS)
-    def _(chunk):
-        spread(chunk)
-
-    pl.semaphore_wait(round_sem.at[1], 6)
-    go(18, NEAR)
+        spread_pair(chunk)
 
     for copy in halos:
         copy.wait()
@@ -292,25 +328,26 @@
 
     beside = near((1, 0, 0))
 
-    @pl.loop(0, NEAR)
+    @pl.loop(0, NEAR, step=2)
     def _(chunk):
-        forward_ids(chunk, beside).wait_recv()
-        forward(chunk, beside).wait_recv()
-        spread(chunk)
+        for i in range(2):
+            forward_ids(chunk + i, beside).wait_recv()
+            forward(chunk + i, beside).wait_recv()
+        spread_pair(chunk)
 
     for k in range(3):
-        low_grid[k] = (vel_ref[:, k] + grid_ref[:, k]).reshape(256, 128).astype(BF16)
-
-    def sample(chunk, result):
+        low_grid[k] = grid_ref[:, k].reshape(256, 128).astype(BF16)
+
+    def sample(chunk, result, slot):
         pick_rows = jnp.concatenate([picks[chunk, 0], picks[chunk, 1]], axis=1)
         u = dot(pick_rows, jnp.concatenate([low_grid[k] for k in range(3)], axis=1)).astype(BF16)
         for k in range(3):
-            local_u[:, 16 * k : 16 * k + 16, :] = u[:, 128 * k : 128 * k + 128].reshape(16, 16, 128)
+            local_u[slot, :, 16 * k : 16 * k + 16, :] = u[:, 128 * k : 128 * k + 128].reshape(16, 16, 128)
         for half in range(2):
             sums = [[], [], []]
             for r in range(8 * half, 8 * half + 8):
                 line = jnp.concatenate([along[chunk, r, 0], along[chunk, r, 1]], axis=1)
-                got = dot(local_u[r], line)
+                got = dot(local_u[slot, r], line)
                 weight = across[chunk, r]
                 for k in range(3):
                     value = got[16 * k : 16 * k + 16] * weight
@@ -322,15 +359,18 @@
         offset = offsets_of(chunk)
         return tuple(lax.rem(me[i] - offset[i] + sizes[i], sizes[i]) for i in range(3))
 
-    @pl.loop(0, NEAR)
+    @pl.loop(0, NEAR, step=2)
     def _(turn):
-        chunk = NEAR - 1 - turn
-        sample(chunk, ret_send.at[chunk])
-        back(chunk, origin(chunk)).start()
-
-    @pl.loop(NEAR, CHUNKS)
+        chunk = NEAR - 2 - turn
+        for i in range(2):
+            sample(chunk + i, ret_send.at[chunk + i], i)
+        for i in range(2):
+            back(chunk + i, origin(chunk + i)).start()
+
+    @pl.loop(NEAR, CHUNKS, step=2)
     def _(chunk):
-        sample(chunk, ret_recv.at[chunk])
+        for i in range(2):
+            sample(chunk + i, ret_recv.at[chunk + i], i)
 
     @pl.loop(0, NEAR)
     def _(chunk):
@@ -344,6 +384,11 @@
         high = terms.astype(BF16)
         low = (terms - high.astype(F32)).astype(BF16)
         out_ref[k] = dot(gather, high) + dot(gather, low)
+
+
+def pass_on(grid_in, markers_in, grid_ref, out_ref):
+    grid_ref[...] = grid_in[...]
+    out_ref[...] = markers_in[...]
 
 
 def body(sizes, velocity, marker_pos, marker_force, intersect, tiles):
@@ -355,9 +400,16 @@
             jax.ShapeDtypeStruct((16, 3, 16, 128), F32),
             jax.ShapeDtypeStruct((3, 64, 256), F32),
         ),
-        in_specs=[vmem] * 5,
+        in_specs=[pl.BlockSpec(memory_space=pl.ANY)] * 5,
         out_specs=(vmem, vmem),
         scratch_shapes=[
+            pltpu.VMEM((16, 3, 16, 128), F32),
+            pltpu.VMEM((3, 64, 256), F32),
+            pltpu.VMEM((3, 64, 256), F32),
+            pltpu.VMEM((27, 64), jnp.int32),
+            pltpu.VMEM((27, 16, 64), jnp.int32),
+            dma((5,)),
+            pltpu.VMEM((6, 192, 256), BF16),
             pltpu.VMEM((NEAR, 96, 256), F32),
             pltpu.VMEM((CHUNKS, 96, 256), F32),
             pltpu.VMEM((NEAR, 1, 256), F32),
@@ -366,9 +418,9 @@
             pltpu.VMEM((CHUNKS, CAP, CAP, 256), F32),
             pltpu.VMEM((CHUNKS, 2, 256, 128), BF16),
             pltpu.VMEM((128, 512), BF16),
+            pltpu.VMEM((2, 3, 256, 128), BF16),
             pltpu.VMEM((3, 256, 128), BF16),
-            pltpu.VMEM((3, 256, 128), BF16),
-            pltpu.VMEM((CAP, 48, 128), BF16),
+            pltpu.VMEM((2, CAP, 48, 128), BF16),
             pltpu.VMEM((NEAR, 3, CAP, 256), F32),
             pltpu.VMEM((CHUNKS, 3, CAP, 256), F32),
             pltpu.VMEM((2, 3, CAP, 128), F32),
@@ -396,7 +448,16 @@
         intersect.T,
         jnp.transpose(tiles, (1, 2, 0)),
     )
-    return velocity + jnp.transpose(grid, (0, 2, 1, 3)), jnp.transpose(markers, (1, 0, 2))
+    grid, markers = pl.pallas_call(
+        pass_on,
+        out_shape=(
+            jax.ShapeDtypeStruct((16, 3, 16, 128), F32),
+            jax.ShapeDtypeStruct((3, 64, 256), F32),
+        ),
+        in_specs=[vmem] * 2,
+        out_specs=(vmem, vmem),
+    )(grid, markers)
+    return jnp.transpose(grid, (0, 2, 1, 3)), jnp.transpose(markers, (1, 0, 2))
 
 
 def solution(mesh):

time: 59.7 us -> 54.6 us (0.915)
  Pallas kernels: 56.3 us -> 53.8 us
  other arithmetic: 1.95 us -> 0 us
  local copies, waits for them, and re-layouts: 0.68 us -> 0 us
    pallas_call x1, Pallas kernels: 56.3 us -> 51.9 us  [body(): pl.pallas_call(functools.partial(kernel, sizes), out_shape=(jax.ShapeDtyp...]
    add x1 -> x0, other arithmetic: 1.95 us -> none  [body(): velocity + jnp.transpose(grid, (0, 2, 1, 3))]
    pallas_call x0 -> x1, Pallas kernels: none -> 1.88 us  [body(): pl.pallas_call(pass_on, out_shape=(jax.ShapeDtypeStruct((16, 3, 16, 128),...]
    unnamed x3 -> x0, local copies, waits for them, and re-layouts: 0.68 us -> none
where the time goes in v3:
time: 54.6 us; the launch traced here: 54.4 us
  Pallas kernels  53.8 us (99%)
  between operations  0.64 us (1%)
    pallas_call x1, Pallas kernels, body(): pl.pallas_call(functools.partial(kernel, sizes), out_shape=(jax.ShapeDtyp...  51.9 us
    pallas_call x1, Pallas kernels, body(): pl.pallas_call(pass_on, out_shape=(jax.ShapeDtypeStruct((16, 3, 16, 128),...  1.88 us

profile of v3, /device:TPU:1, one launch (start us, length us, event | category | flops | bytes accessed | tf_op | source)
XLA Modules:
  0.0 54.4 jit_solution(2200949293787562489)
XLA Ops:
  0.6 51.9 %shard_map.68 = (f32[16,3,16,128]{3,2,1,0:T(8,128)}, f32[3,64,256]{2,1,0:T(8,128)}) custom-call(f32[16,3,16,128]{3,2,1,0:T(8,128)} %bitcast.7, f32[3,64,256]{2,1,0:T(8,128)} %bitcast.9, f32[3,64,256]{2,1,0:T(8,128)} %bitcast.10, s32[27,64]{1,0:T(8,128)} %bitcast.11, s32[27,16,64]{2,1,0:T(8,128)} %bitcast.8), custom_call_target="tpu_custom_call" | custom-call | tf_op jit(solution)/shard_map/pallas_call | solution.py:397
  52.5 1.9 %shard_map.69 = (f32[16,3,16,128]{3,2,1,0:T(8,128)}, f32[3,64,256]{2,1,0:T(8,128)}) custom-call(f32[16,3,16,128]{3,2,1,0:T(8,128)} %get-tuple-element.6.grid_in, f32[3,64,256]{2,1,0:T(8,128)} %get-tuple-element.7.markers_in), custom_call_target="tpu_custom_call" | custom-call | tf_op jit(solution)/shard_map/pallas_call | solution.py:451

commit v4 on v3

--- a/solution.py
+++ b/solution.py
@@ -88,8 +88,8 @@
 
 
 def kernel(
-    sizes, vel_in, pos_in, force_in, flag_in, tile_in, grid_ref, out_ref,
-    vel_ref, pos_ref, force_ref, flag_ref, tile_ref, in_sem, split,
+    sizes, vel_in, pos_in, force_in, flag_in, tile_in, grid_out, out_ref,
+    grid_ref, out_sem, vel_ref, pos_ref, force_ref, flag_ref, tile_ref, in_sem, split,
     send, recv, send_ids, recv_ids, along, across, picks, gather_t, pieces, low_grid, local_u, ret_send, ret_recv,
     face_y_send, face_z_send, face_x, face_y, face_z,
     round_sem, send_sem, recv_sem, isend_sem, irecv_sem, rsend_sem, rrecv_sem, hsend_sem, hrecv_sem,
@@ -338,11 +338,18 @@
     for k in range(3):
         low_grid[k] = grid_ref[:, k].reshape(256, 128).astype(BF16)
 
-    def sample(chunk, result, slot):
-        pick_rows = jnp.concatenate([picks[chunk, 0], picks[chunk, 1]], axis=1)
+    grid_copy = pltpu.make_async_copy(grid_ref, grid_out, out_sem)
+    grid_copy.start()
+
+    def fetch(chunk):
+        pick_rows = jnp.concatenate(
+            [jnp.concatenate([picks[chunk + i, 0], picks[chunk + i, 1]], axis=1) for i in range(2)], axis=0
+        )
         u = dot(pick_rows, jnp.concatenate([low_grid[k] for k in range(3)], axis=1)).astype(BF16)
         for k in range(3):
-            local_u[slot, :, 16 * k : 16 * k + 16, :] = u[:, 128 * k : 128 * k + 128].reshape(16, 16, 128)
+            local_u[:, :, 16 * k : 16 * k + 16, :] = u[:, 128 * k : 128 * k + 128].reshape(2, 16, 16, 128)
+
+    def sample(chunk, result, slot):
         for half in range(2):
             sums = [[], [], []]
             for r in range(8 * half, 8 * half + 8):
@@ -362,6 +369,7 @@
     @pl.loop(0, NEAR, step=2)
     def _(turn):
         chunk = NEAR - 2 - turn
+        fetch(chunk)
         for i in range(2):
             sample(chunk + i, ret_send.at[chunk + i], i)
         for i in range(2):
@@ -369,6 +377,7 @@
 
     @pl.loop(NEAR, CHUNKS, step=2)
     def _(chunk):
+        fetch(chunk)
         for i in range(2):
             sample(chunk + i, ret_recv.at[chunk + i], i)
 
@@ -376,19 +385,47 @@
     def _(chunk):
         forward_ids(chunk, beside).wait_send()
         forward(chunk, beside).wait_send()
+
+    def take(low, high):
+        gather = gather_t[0:64, low * CAP : high * CAP]
+        result = []
+        for k in range(3):
+            terms = ret_recv[low:high, k].reshape((high - low) * CAP, 256)
+            top = terms.astype(BF16)
+            rest_part = (terms - top.astype(F32)).astype(BF16)
+            result.append(dot(gather, top) + dot(gather, rest_part))
+        return result
+
+    @pl.loop(8, NEAR)
+    def _(chunk):
         back(chunk, beside).wait()
 
-    gather = gather_t[0:64, 0:rows]
+    early = take(8, CHUNKS)
     for k in range(3):
-        terms = ret_recv[:, k].reshape(rows, 256)
-        high = terms.astype(BF16)
-        low = (terms - high.astype(F32)).astype(BF16)
-        out_ref[k] = dot(gather, high) + dot(gather, low)
-
-
-def pass_on(grid_in, markers_in, grid_ref, out_ref):
-    grid_ref[...] = grid_in[...]
-    out_ref[...] = markers_in[...]
+        out_ref[k] = early[k]
+
+    @pl.loop(0, 8)
+    def _(chunk):
+        back(chunk, beside).wait()
+
+    late = take(0, 8)
+    for k in range(3):
+        out_ref[k] += late[k]
+    grid_copy.wait()
+
+
+def pass_on(grid_in, markers_in, grid_out, markers_out, grid, markers, in_sem, out_sem):
+    pieces = [(grid_in.at[4 * i : 4 * i + 4], grid.at[4 * i : 4 * i + 4], grid_out.at[4 * i : 4 * i + 4]) for i in range(4)]
+    pieces += [(markers_in.at[k], markers.at[k], markers_out.at[k]) for k in range(3)]
+    loads = [pltpu.make_async_copy(a, b, in_sem.at[i]) for i, (a, b, _) in enumerate(pieces)]
+    stores = [pltpu.make_async_copy(b, c, out_sem.at[i]) for i, (_, b, c) in enumerate(pieces)]
+    for load in loads:
+        load.start()
+    for load, store in zip(loads, stores):
+        load.wait()
+        store.start()
+    for store in stores:
+        store.wait()
 
 
 def body(sizes, velocity, marker_pos, marker_force, intersect, tiles):
@@ -401,8 +438,10 @@
             jax.ShapeDtypeStruct((3, 64, 256), F32),
         ),
         in_specs=[pl.BlockSpec(memory_space=pl.ANY)] * 5,
-        out_specs=(vmem, vmem),
+        out_specs=(pl.BlockSpec(memory_space=pl.ANY), vmem),
         scratch_shapes=[
+            pltpu.VMEM((16, 3, 16, 128), F32),
+            pltpu.SemaphoreType.DMA,
             pltpu.VMEM((16, 3, 16, 128), F32),
             pltpu.VMEM((3, 64, 256), F32),
             pltpu.VMEM((3, 64, 256), F32),
@@ -454,8 +493,14 @@
             jax.ShapeDtypeStruct((16, 3, 16, 128), F32),
             jax.ShapeDtypeStruct((3, 64, 256), F32),
         ),
-        in_specs=[vmem] * 2,
-        out_specs=(vmem, vmem),
+        in_specs=[pl.BlockSpec(memory_space=pl.ANY)] * 2,
+        out_specs=(pl.BlockSpec(memory_space=pl.ANY), pl.BlockSpec(memory_space=pl.ANY)),
+        scratch_shapes=[
+            pltpu.VMEM((16, 3, 16, 128), F32),
+            pltpu.VMEM((3, 64, 256), F32),
+            dma((7,)),
+            dma((7,)),
+        ],
     )(grid, markers)
     return jnp.transpose(grid, (0, 2, 1, 3)), jnp.transpose(markers, (1, 0, 2))
 

time: 54.6 us -> 53.5 us (0.980)
  Pallas kernels: 53.8 us -> 52.7 us
    pallas_call x1, Pallas kernels: 51.9 us -> 50.8 us  [body(): pl.pallas_call(functools.partial(kernel, sizes), out_shape=(jax.ShapeDtyp...]
where the time goes in v4:
time: 53.5 us; the launch traced here: 53.3 us
  Pallas kernels  52.7 us (99%)
  between operations  0.64 us (1%)
    pallas_call x1, Pallas kernels, body(): pl.pallas_call(functools.partial(kernel, sizes), out_shape=(jax.ShapeDtyp...  50.8 us
    pallas_call x1, Pallas kernels, body(): pl.pallas_call(pass_on, out_shape=(jax.ShapeDtypeStruct((16, 3, 16, 128),...  1.86 us

profile of v4, /device:TPU:1, one launch (start us, length us, event | category | flops | bytes accessed | tf_op | source)
XLA Modules:
  0.0 53.3 jit_solution(1159593759675509756)
XLA Ops:
  0.6 50.8 %shard_map.68 = (f32[16,3,16,128]{3,2,1,0:T(8,128)}, f32[3,64,256]{2,1,0:T(8,128)}) custom-call(f32[16,3,16,128]{3,2,1,0:T(8,128)} %bitcast.7, f32[3,64,256]{2,1,0:T(8,128)} %bitcast.9, f32[3,64,256]{2,1,0:T(8,128)} %bitcast.10, s32[27,64]{1,0:T(8,128)} %bitcast.11, s32[27,16,64]{2,1,0:T(8,128)} %bitcast.8), custom_call_target="tpu_custom_call" | custom-call | tf_op jit(solution)/shard_map/pallas_call | solution.py:434
  51.5 1.9 %shard_map.69 = (f32[16,3,16,128]{3,2,1,0:T(8,128)}, f32[3,64,256]{2,1,0:T(8,128)}) custom-call(f32[16,3,16,128]{3,2,1,0:T(8,128)} %get-tuple-element.6.grid_in, f32[3,64,256]{2,1,0:T(8,128)} %get-tuple-element.7.markers_in), custom_call_target="tpu_custom_call" | custom-call | tf_op jit(solution)/shard_map/pallas_call | solution.py:490

commit v5 on v4

--- a/solution.py
+++ b/solution.py
@@ -19,10 +19,7 @@
 
 
 FACES = [(1, 0, 0), (0, 0, 1), (0, 1, 0), (-1, 0, 0), (0, 0, -1), (0, -1, 0)]
-EDGES = [
-    (1, 0, 1), (0, 1, -1), (-1, 1, 0), (0, -1, 1), (-1, 0, -1), (1, -1, 0),
-    (1, 1, 0), (0, -1, -1), (-1, 0, 1), (0, 1, 1), (1, 0, -1), (-1, -1, 0),
-]
+EDGES = [(0, 1, 1), (0, -1, -1), (0, 1, -1), (0, -1, 1), (1, 0, 1), (-1, 1, 0), (-1, 0, -1), (1, -1, 0), (-1, 0, 1), (1, 1, 0), (1, 0, -1), (-1, -1, 0)]
 CORNERS = [
     (1, 1, 1), (-1, -1, -1), (1, -1, 1), (-1, 1, -1), (-1, 1, 1), (1, -1, -1), (1, 1, -1), (-1, -1, 1),
 ]

time: 53.5 us -> 53.1 us (level)
  Pallas kernels: 52.7 us -> 52 us
    pallas_call x1, Pallas kernels: 50.8 us -> 50.1 us  [body(): pl.pallas_call(functools.partial(kernel, sizes), out_shape=(jax.ShapeDtyp...]
where the time goes in v5:
time: 53.1 us; the launch traced here: 52.6 us
  Pallas kernels  52 us (98%)
  between operations  0.64 us (1%)
    pallas_call x1, Pallas kernels, body(): pl.pallas_call(functools.partial(kernel, sizes), out_shape=(jax.ShapeDtyp...  50.1 us
    pallas_call x1, Pallas kernels, body(): pl.pallas_call(pass_on, out_shape=(jax.ShapeDtypeStruct((16, 3, 16, 128),...  1.86 us

profile of v5, /device:TPU:1, one launch (start us, length us, event | category | flops | bytes accessed | tf_op | source)
XLA Modules:
  0.0 52.6 jit_solution(5709921502683078112)
XLA Ops:
  0.6 50.1 %shard_map.68 = (f32[16,3,16,128]{3,2,1,0:T(8,128)}, f32[3,64,256]{2,1,0:T(8,128)}) custom-call(f32[16,3,16,128]{3,2,1,0:T(8,128)} %bitcast.7, f32[3,64,256]{2,1,0:T(8,128)} %bitcast.9, f32[3,64,256]{2,1,0:T(8,128)} %bitcast.10, s32[27,64]{1,0:T(8,128)} %bitcast.11, s32[27,16,64]{2,1,0:T(8,128)} %bitcast.8), custom_call_target="tpu_custom_call" | custom-call | tf_op jit(solution)/shard_map/pallas_call | solution.py:431
  50.7 1.9 %shard_map.69 = (f32[16,3,16,128]{3,2,1,0:T(8,128)}, f32[3,64,256]{2,1,0:T(8,128)}) custom-call(f32[16,3,16,128]{3,2,1,0:T(8,128)} %get-tuple-element.6.grid_in, f32[3,64,256]{2,1,0:T(8,128)} %get-tuple-element.7.markers_in), custom_call_target="tpu_custom_call" | custom-call | tf_op jit(solution)/shard_map/pallas_call | solution.py:487
